TPU v7x, 128 devices: a whole 4x4x4 slice. The times are simulated.
128 devices in a mesh: row: 16 (over z, x), col: 8 (over y, core).
Axes of the slice: x: 4, y: 4, z: 4, core: 2. Of those that a mesh axis runs over, the one named last changes fastest.
Arguments:
- start_block: float32 [8, 131072], P(None, ('row', 'col')), may hold values from -6 to 6
- blocks: bfloat16 [16, 8, 128, 128, 128], P('row', 'col'), as said below
- block_rows: int32 [16, 8, 128], P(None, 'col'), may hold values from 0 to 63, as said below
- block_cols: int32 [16, 8, 128], P(None, 'col'), may hold values from 0 to 127, as said below
- counts: int32 [16, 8], replicated, may hold values from 1 to 128, as said below
Outputs:
- next_block: float32 [8, 131072], P(None, ('row', 'col'))
- tridiagonal: float32 [16, 16], replicated
Inputs may be any that keep to these rules, and one draw needn't show every extreme that they name: `block_rows`: entries of each tile are local block rows below 64; within a tile the used slots name distinct blocks whose global row block is at or after the global column block; slots at or after counts are 0 and not part of H. `block_cols`: local block columns below 128, paired with block_rows; unused slots are 0. `counts`: some tile holds exactly 128 blocks in every draw. Blocks whose global row and column blocks agree are symmetric.
All inputs are finite; a program needn't handle non-finite values.
Results may differ from a plain program's by a relative error of at most 0.0048.
Values may be sent and summed in bfloat16 or wider, within the bound.
A program may use at most 64 MiB of HBM per device.

v0:
```python
import math

import jax
import jax.numpy as jnp
from jax import lax
from jax.sharding import Mesh
from jax.sharding import PartitionSpec as P

ITERS = 2
ROW = ("row_0", "row_1")
COL = ("col_0", "col_1")
ROW_COL = ("row_0", "row_1", "col_0", "col_1")


blocks_per_step = 16


def sent_to_all(value, axis):
    length = lax.axis_size(axis)
    return lax.all_to_all(
        jnp.broadcast_to(value[None], (length, *value.shape)), axis, 0, 0, tiled=True
    )


def joined_along(tiles, dim):
    tiles = jnp.moveaxis(tiles, 0, dim)
    lengths = tiles.shape
    return tiles.reshape(*lengths[:dim], lengths[dim] * lengths[dim + 1], *lengths[dim + 2 :])


def collect(value, axis, dim):
    tiles = sent_to_all(value, axis)
    return joined_along(tiles, dim)


def split_up(value, dim, length):
    lengths = value.shape
    tiles = value.reshape(*lengths[:dim], length, lengths[dim] // length, *lengths[dim + 1 :])
    return jnp.moveaxis(tiles, dim, 0)


def sent_and_summed(value, axis, dim):
    length = lax.axis_size(axis)
    tiles = lax.all_to_all(split_up(value, dim, length), axis, 0, 0, tiled=True)
    return jnp.sum(tiles, axis=0)


def over_axes(value, axes):
    for axis in axes:
        value = lax.psum(value, axis)
    return value


def accumulate(
    stored,
    row_list,
    col_list,
    first_slot,
    live_count,
    tile_row,
    tile_col,
    shape_info,
    row_vector,
    col_vector,
    totals,
):
    row_blocks, col_blocks, piece_blocks, grid_cols = shape_info
    vectors = row_vector.shape[0]
    block_side = stored.shape[-1]
    slot_total = stored.shape[0]
    row_pieces = row_vector.reshape(vectors, row_blocks, block_side)
    col_pieces = col_vector.reshape(vectors, col_blocks, block_side)
    offsets = jnp.arange(blocks_per_step, dtype=jnp.int32)
    row_range = jnp.arange(row_blocks, dtype=jnp.int32)
    col_range = jnp.arange(col_blocks, dtype=jnp.int32)

    def visit(group_index, running):
        row_total, col_total = running
        local_slot = group_index * blocks_per_step + offsets
        is_valid = local_slot < live_count
        slot_ids = jnp.clip(first_slot + local_slot, 0, slot_total - 1)
        tile_data = jnp.take(stored, slot_ids, axis=0)
        row_ids = jnp.take(row_list, slot_ids)
        col_ids = jnp.take(col_list, slot_ids)
        global_row = tile_row * row_blocks + row_ids
        global_col = (
            col_ids // piece_blocks * grid_cols + tile_col
        ) * piece_blocks + col_ids % piece_blocks
        mirror = is_valid & (global_row != global_col)
        col_taken = jnp.take(col_pieces, col_ids, axis=1)
        row_taken = jnp.take(row_pieces, row_ids, axis=1)
        direct = jnp.einsum(
            "gij,kgj->kgi", tile_data, col_taken, preferred_element_type=jnp.float32
        )
        turned = jnp.einsum(
            "gji,kgj->kgi", tile_data, row_taken, preferred_element_type=jnp.float32
        )
        pick_rows = ((row_ids[:, None] == row_range[None, :]) & is_valid[:, None]).astype(
            jnp.float32
        )
        pick_cols = ((col_ids[:, None] == col_range[None, :]) & mirror[:, None]).astype(jnp.float32)
        row_total = row_total + jnp.einsum(
            "gs,kgi->ksi", pick_rows, direct, precision=lax.Precision.HIGHEST
        )
        col_total = col_total + jnp.einsum(
            "gs,kgi->ksi", pick_cols, turned, precision=lax.Precision.HIGHEST
        )
        return (row_total, col_total)

    group_count = (live_count + blocks_per_step - 1) // blocks_per_step
    return lax.fori_loop(0, group_count, visit, totals)


def per_device(start_block, blocks, block_rows, block_cols, counts):
    highest = lax.Precision.HIGHEST
    vectors, piece_len = start_block.shape
    stored = blocks[0, 0]
    block_side = stored.shape[-1]
    grid_rows = lax.axis_size(ROW)
    grid_cols = lax.axis_size(COL)
    piece_blocks = piece_len // block_side
    row_blocks = grid_cols * piece_blocks
    col_blocks = grid_rows * piece_blocks
    shape_info = (row_blocks, col_blocks, piece_blocks, grid_cols)
    tile_row = lax.axis_index(ROW)
    tile_col = lax.axis_index(COL)
    row_lists = block_rows[:, 0, :]
    col_lists = block_cols[:, 0, :]
    own_count = counts[tile_row, tile_col]
    own_rows = row_lists[tile_row]
    own_cols = col_lists[tile_row]
    start_sum = over_axes(jnp.dot(start_block, start_block.T, precision=highest), ROW_COL)
    factor = jnp.linalg.cholesky(start_sum)
    current = lax.linalg.triangular_solve(factor, start_block, left_side=True, lower=True)
    previous = current
    prev_factor = factor
    diagonals = []
    couplings = []
    for step_index in range(ITERS):
        half_block = current.astype(jnp.bfloat16)
        row_vector = collect(half_block, COL, 1)
        col_vector = collect(half_block, ROW, 1)
        row_zero = jnp.zeros((vectors, row_blocks, block_side), jnp.float32)
        col_zero = jnp.zeros((vectors, col_blocks, block_side), jnp.float32)
        row_total, col_total = accumulate(
            stored,
            own_rows,
            own_cols,
            0,
            own_count,
            tile_row,
            tile_col,
            shape_info,
            row_vector,
            col_vector,
            (row_zero, col_zero),
        )
        row_part = sent_and_summed(row_total.reshape(vectors, row_blocks * block_side), COL, 1)
        col_part = sent_and_summed(col_total.reshape(vectors, col_blocks * block_side), ROW, 1)
        image = row_part + col_part
        if step_index > 0:
            image = image - jnp.dot(prev_factor.T, previous, precision=highest)
        local_proj = jnp.dot(current, image.T, precision=highest)
        local_square = jnp.dot(image, image.T, precision=highest)
        projection, squares = (over_axes(local_proj, ROW_COL), over_axes(local_square, ROW_COL))
        image = image - jnp.dot(projection.T, current, precision=highest)
        gram = squares - jnp.dot(projection.T, projection, precision=highest)
        factor = jnp.linalg.cholesky(gram)
        following = lax.linalg.triangular_solve(factor, image, left_side=True, lower=True)
        diagonals.append(projection)
        couplings.append(factor)
        previous, prev_factor, current = (current, factor, following)
    tri_size = ITERS * vectors
    tridiagonal = jnp.zeros((tri_size, tri_size), jnp.float32)
    for step_index in range(ITERS):
        low = step_index * vectors
        tridiagonal = tridiagonal.at[low : low + vectors, low : low + vectors].set(
            diagonals[step_index]
        )
        if step_index + 1 < ITERS:
            tridiagonal = tridiagonal.at[
                low : low + vectors, low + vectors : low + 2 * vectors
            ].set(couplings[step_index])
            tridiagonal = tridiagonal.at[
                low + vectors : low + 2 * vectors, low : low + vectors
            ].set(couplings[step_index].T)
    order_root = math.sqrt(piece_len * grid_rows * grid_cols)
    return (current * order_root, tridiagonal)


def solution(mesh):
    torus = Mesh(mesh.devices.reshape(4, 4, 4, 2), ("row_0", "row_1", "col_0", "col_1"))
    return jax.shard_map(
        per_device,
        mesh=torus,
        in_specs=(
            P(None, ROW_COL),
            P(ROW, COL, None, None, None),
            P(None, COL, None),
            P(None, COL, None),
            P(),
        ),
        out_specs=(P(None, ROW_COL), P()),
        check_vma=False,
    )
```

profile of v0, /device:TPU:1, one launch (start us, length us, event | category | flops | bytes accessed | tf_op | source)
XLA Modules:
  0.0 333.4 jit_solution(16994987881674295431)
XLA Ops:
  0.6 0.7 copy-done
  1.5 10.6 %psum.140 = f32[8,8]{0,1:T(8,128)S(1)} all-reduce(f32[8,8]{0,1:T(8,128)S(1)} %fusion.92), channel_id=1, replica_groups=mesh['row_0'=4,'row_1'=4,'col_0'=4,'col_1'=2] {'row_0'}, use_global_device_ids=true, to_apply=%region_0.0 | all-reduce | flops 64 | bytes 512 | tf_op jit(solution)/shard_map/psum | solution.py:50
  12.1 8.8 %psum.141 = f32[8,8]{0,1:T(8,128)S(1)} all-reduce(f32[8,8]{0,1:T(8,128)S(1)} %psum.140), channel_id=1, replica_groups=mesh['row_0'=4,'row_1'=4,'col_0'=4,'col_1'=2] {'row_1'}, use_global_device_ids=true, to_apply=%region_1.0 | all-reduce | flops 64 | bytes 512 | tf_op jit(solution)/shard_map/psum | solution.py:50
  20.9 8.7 %psum.142 = f32[8,8]{0,1:T(8,128)S(1)} all-reduce(f32[8,8]{0,1:T(8,128)S(1)} %psum.141), channel_id=1, replica_groups=mesh['row_0'=4,'row_1'=4,'col_0'=4,'col_1'=2] {'col_0'}, use_global_device_ids=true, to_apply=%region_2.0 | all-reduce | flops 64 | bytes 512 | tf_op jit(solution)/shard_map/psum | solution.py:50
  29.6 8.6 %psum.143 = f32[8,8]{0,1:T(8,128)S(1)} all-reduce(f32[8,8]{0,1:T(8,128)S(1)} %psum.142), channel_id=1, replica_groups=mesh['row_0'=4,'row_1'=4,'col_0'=4,'col_1'=2] {'col_1'}, use_global_device_ids=true, to_apply=%region_3.0 | all-reduce | flops 64 | bytes 512 | tf_op jit(solution)/shard_map/psum | solution.py:50
  38.2 0.7 cholesky.59
  41.2 8.0 %all_to_all.40 = bf16[8,8,1024]{2,1,0:T(8,128)(2,1)S(1)} all-to-all(bf16[8,8,1024]{2,1,0:T(8,128)(2,1)S(1)} %broadcast_in_dim.46), channel_id=1, replica_groups=mesh['row_0'=4,'row_1'=4,'col_0'=4,'col_1'=2] {'col_0','col_1'}, dimensions={0} | all-to-all | bytes 262144 | tf_op jit(solution)/shard_map/all_to_all | solution.py:20
  49.1 0.7 broadcast_in_dim.45
  49.9 3.5 %all-to-all-start = ((bf16[16,8,1024]{2,1,0:T(8,128)(2,1)}), bf16[16,8,1024]{2,1,0:T(8,128)(2,1)S(1)}, u32[]{:S(2)}, u32[]{:S(2)}) async-start(bf16[16,8,1024]{2,1,0:T(8,128)(2,1)} %broadcast_in_dim.45), calls=%async_computation | async-start | bytes 524288 | tf_op jit(solution)/shard_map/all_to_all | solution.py:20
  53.4 1.3 dynamic_slice.9
  55.4 0.7 dynamic-slice_bitcast_fusion
  56.1 5.2 %all-to-all-done = bf16[16,8,1024]{2,1,0:T(8,128)(2,1)S(1)} async-done(((bf16[16,8,1024]{2,1,0:T(8,128)(2,1)}), bf16[16,8,1024]{2,1,0:T(8,128)(2,1)S(1)}, u32[]{:S(2)}, u32[]{:S(2)}) %all-to-all-start) | async-done | bytes 262176 | tf_op jit(solution)/shard_map/all_to_all | solution.py:20
  61.3 8.0 %while.34 = (s32[]{:T(128)}, f32[8,64,128]{2,1,0:T(8,128)S(1)}, f32[8,128,128]{1,2,0:T(8,128)S(1)}, s32[]{:T(128)}, s32[128]{0:T(128)S(1)}, /*index=5*/bf16[8,12...) while((s32[]{:T(128)}, f32[8,64,128]{2,1,0:T(8,128)S(1)}, ...), condition=%wide.region_7.14_spmd.clone, body=%wide.region_6.13_spmd.clone.sunk | while | flops 46901184 | bytes 4142997 | solution.py:111
  64.6 2.8 gather_fusion
  69.4 0.9 copy.60
  70.3 5.0 %all-to-all-start.2 = ((f32[8,8,1024]{2,1,0:T(8,128)}), f32[8,8,1024]{2,1,0:T(8,128)S(1)}, u32[]{:S(2)}, u32[]{:S(2)}) async-start(f32[8,8,1024]{2,1,0:T(8,128)} %copy.60), calls=%async_computation.2 | async-start | bytes 524288 | tf_op jit(solution)/shard_map/all_to_all | solution.py:44
  75.6 1.1 copy.62
  76.7 5.1 %all-to-all-done.2 = f32[8,8,1024]{2,1,0:T(8,128)S(1)} async-done(((f32[8,8,1024]{2,1,0:T(8,128)}), f32[8,8,1024]{2,1,0:T(8,128)S(1)}, u32[]{:S(2)}, u32[]{:S(2)}) %all-to-all-start.2) | async-done | bytes 262176 | tf_op jit(solution)/shard_map/all_to_all | solution.py:44
  81.8 58.6 %all-to-all-start.3 = ((f32[16,8,1024]{2,1,0:T(8,128)}), f32[16,8,1024]{2,1,0:T(8,128)S(1)}, u32[]{:S(2)}, u32[]{:S(2)}) async-start(f32[16,8,1024]{2,1,0:T(8,128)} %copy.62), calls=%async_computation.3 | async-start | bytes 1048576 | tf_op jit(solution)/shard_map/all_to_all | solution.py:44
  141.7 9.1 %all-to-all-done.3 = f32[16,8,1024]{2,1,0:T(8,128)S(1)} async-done(((f32[16,8,1024]{2,1,0:T(8,128)}), f32[16,8,1024]{2,1,0:T(8,128)S(1)}, u32[]{:S(2)}, u32[]{:S(2)}) %all-to-all-start.3) | async-done | bytes 524320 | tf_op jit(solution)/shard_map/all_to_all | solution.py:44
  151.1 6.7 %all-reduce.6 = (f32[8,8]{1,0:T(8,128)S(1)}, f32[8,8]{0,1:T(8,128)S(1)}) all-reduce(f32[8,8]{1,0:T(8,128)S(1)} %fusion.94, f32[8,8]{0,1:T(8,128)S(1)} %fusion.93), channel_id=1, replica_groups=mesh['row_0'=4,'row_1'=4,'col_0'=4,'col_1'=2] {'row_0'}, use_global_device_ids=true, to_apply=%region_14.21 | all-reduce | flops 128 | bytes 1024 | tf_op jit(solution)/shard_map/psum | solution.py:50
  157.9 6.7 %all-reduce.4 = (f32[8,8]{1,0:T(8,128)S(1)}, f32[8,8]{0,1:T(8,128)S(1)}) all-reduce(f32[8,8]{1,0:T(8,128)S(1)} %get-tuple-element.564, f32[8,8]{0,1:T(8,128)S(1)} %get-tuple-element.565), channel_id=1, replica_groups=mesh['row_0'=4,'row_1'=4,'col_0'=4,'col_1'=2] {'row_1'}, use_global_device_ids=true, to_apply=%region_15.22 | all-reduce | flops 128 | bytes 1024 | tf_op jit(solution)/shard_map/psum | solution.py:50
  164.6 7.0 %all-reduce.2 = (f32[8,8]{1,0:T(8,128)S(1)}, f32[8,8]{0,1:T(8,128)S(1)}) all-reduce(f32[8,8]{1,0:T(8,128)S(1)} %get-tuple-element.560, f32[8,8]{0,1:T(8,128)S(1)} %get-tuple-element.561), channel_id=1, replica_groups=mesh['row_0'=4,'row_1'=4,'col_0'=4,'col_1'=2] {'col_0'}, use_global_device_ids=true, to_apply=%region_16.23 | all-reduce | flops 128 | bytes 1024 | tf_op jit(solution)/shard_map/psum | solution.py:50
  171.5 10.3 %all-reduce.8 = (f32[8,8]{1,0:T(8,128)S(1)}, f32[8,8]{0,1:T(8,128)S(1)}) all-reduce(f32[8,8]{1,0:T(8,128)S(1)} %get-tuple-element.556, f32[8,8]{0,1:T(8,128)S(1)} %get-tuple-element.557), channel_id=1, replica_groups=mesh['row_0'=4,'row_1'=4,'col_0'=4,'col_1'=2] {'col_1'}, use_global_device_ids=true, to_apply=%region_17.24 | all-reduce | flops 128 | bytes 1024 | tf_op jit(solution)/shard_map/psum | solution.py:50
  182.4 0.7 cholesky.70
  183.2 0.7 compare_reduce_fusion.1
  183.9 2.6 fusion.83
  187.3 8.0 %all_to_all.41 = bf16[8,8,1024]{2,1,0:T(8,128)(2,1)S(1)} all-to-all(bf16[8,8,1024]{2,1,0:T(8,128)(2,1)S(1)} %broadcast_in_dim.48), channel_id=1, replica_groups=mesh['row_0'=4,'row_1'=4,'col_0'=4,'col_1'=2] {'col_0','col_1'}, dimensions={0} | all-to-all | bytes 262144 | tf_op jit(solution)/shard_map/all_to_all | solution.py:20
  195.3 0.7 broadcast_in_dim.47
  196.0 3.5 %all-to-all-start.4 = ((bf16[16,8,1024]{2,1,0:T(8,128)(2,1)}), bf16[16,8,1024]{2,1,0:T(8,128)(2,1)S(1)}, u32[]{:S(2)}, u32[]{:S(2)}) async-start(bf16[16,8,1024]{2,1,0:T(8,128)(2,1)} %broadcast_in_dim.47), calls=%async_computation.4 | async-start | bytes 524288 | tf_op jit(solution)/shard_map/all_to_all | solution.py:20
  199.6 7.9 %all-to-all-done.4 = bf16[16,8,1024]{2,1,0:T(8,128)(2,1)S(1)} async-done(((bf16[16,8,1024]{2,1,0:T(8,128)(2,1)}), bf16[16,8,1024]{2,1,0:T(8,128)(2,1)S(1)}, u32[]{:S(2)}, u32[]{:S(2)}) %all-to-all-start.4) | async-done | bytes 262176 | tf_op jit(solution)/shard_map/all_to_all | solution.py:20
  207.5 8.0 %while.35 = (s32[]{:T(128)}, f32[8,64,128]{2,1,0:T(8,128)S(1)}, f32[8,128,128]{1,2,0:T(8,128)S(1)}, s32[]{:T(128)}, s32[128]{0:T(128)S(1)}, /*index=5*/bf16[8,12...) while((s32[]{:T(128)}, f32[8,64,128]{2,1,0:T(8,128)S(1)}, ...), condition=%wide.region_19.26_spmd.clone, body=%wide.region_18.25_spmd.clone.sunk | while | flops 46901184 | bytes 4142997 | solution.py:111
  210.8 2.8 gather_fusion.5
  214.8 0.7 fusion.150
  215.6 0.9 copy.67
  216.4 5.0 %all-to-all-start.6 = ((f32[8,8,1024]{2,1,0:T(8,128)}), f32[8,8,1024]{2,1,0:T(8,128)S(1)}, u32[]{:S(2)}, u32[]{:S(2)}) async-start(f32[8,8,1024]{2,1,0:T(8,128)} %copy.67), calls=%async_computation.6 | async-start | bytes 524288 | tf_op jit(solution)/shard_map/all_to_all | solution.py:44
  221.8 1.1 copy.69
  222.9 5.1 %all-to-all-done.6 = f32[8,8,1024]{2,1,0:T(8,128)S(1)} async-done(((f32[8,8,1024]{2,1,0:T(8,128)}), f32[8,8,1024]{2,1,0:T(8,128)S(1)}, u32[]{:S(2)}, u32[]{:S(2)}) %all-to-all-start.6) | async-done | bytes 262176 | tf_op jit(solution)/shard_map/all_to_all | solution.py:44
  228.0 58.6 %all-to-all-start.7 = ((f32[16,8,1024]{2,1,0:T(8,128)}), f32[16,8,1024]{2,1,0:T(8,128)S(1)}, u32[]{:S(2)}, u32[]{:S(2)}) async-start(f32[16,8,1024]{2,1,0:T(8,128)} %copy.69), calls=%async_computation.7 | async-start | bytes 1048576 | tf_op jit(solution)/shard_map/all_to_all | solution.py:44
  286.7 1.8 scatter.15
  288.9 8.0 %all-to-all-done.7 = f32[16,8,1024]{2,1,0:T(8,128)S(1)} async-done(((f32[16,8,1024]{2,1,0:T(8,128)}), f32[16,8,1024]{2,1,0:T(8,128)S(1)}, u32[]{:S(2)}, u32[]{:S(2)}) %all-to-all-start.7) | async-done | bytes 524320 | tf_op jit(solution)/shard_map/all_to_all | solution.py:44
  297.0 0.8 convolution_subtract_fusion.1
  298.2 6.7 %all-reduce.5 = (f32[8,8]{1,0:T(8,128)S(1)}, f32[8,8]{0,1:T(8,128)S(1)}) all-reduce(f32[8,8]{1,0:T(8,128)S(1)} %fusion.96, f32[8,8]{0,1:T(8,128)S(1)} %fusion.95), channel_id=1, replica_groups=mesh['row_0'=4,'row_1'=4,'col_0'=4,'col_1'=2] {'row_0'}, use_global_device_ids=true, to_apply=%region_26.33 | all-reduce | flops 128 | bytes 1024 | tf_op jit(solution)/shard_map/psum | solution.py:50
  304.9 6.7 %all-reduce.3 = (f32[8,8]{1,0:T(8,128)S(1)}, f32[8,8]{0,1:T(8,128)S(1)}) all-reduce(f32[8,8]{1,0:T(8,128)S(1)} %get-tuple-element.562, f32[8,8]{0,1:T(8,128)S(1)} %get-tuple-element.563), channel_id=1, replica_groups=mesh['row_0'=4,'row_1'=4,'col_0'=4,'col_1'=2] {'row_1'}, use_global_device_ids=true, to_apply=%region_27.34 | all-reduce | flops 128 | bytes 1024 | tf_op jit(solution)/shard_map/psum | solution.py:50
  311.6 7.0 %all-reduce.1 = (f32[8,8]{1,0:T(8,128)S(1)}, f32[8,8]{0,1:T(8,128)S(1)}) all-reduce(f32[8,8]{1,0:T(8,128)S(1)} %get-tuple-element.558, f32[8,8]{0,1:T(8,128)S(1)} %get-tuple-element.559), channel_id=1, replica_groups=mesh['row_0'=4,'row_1'=4,'col_0'=4,'col_1'=2] {'col_0'}, use_global_device_ids=true, to_apply=%region_28.35 | all-reduce | flops 128 | bytes 1024 | tf_op jit(solution)/shard_map/psum | solution.py:50
  318.5 10.3 %all-reduce.7 = (f32[8,8]{1,0:T(8,128)S(1)}, f32[8,8]{0,1:T(8,128)S(1)}) all-reduce(f32[8,8]{1,0:T(8,128)S(1)} %get-tuple-element.554, f32[8,8]{0,1:T(8,128)S(1)} %get-tuple-element.555), channel_id=1, replica_groups=mesh['row_0'=4,'row_1'=4,'col_0'=4,'col_1'=2] {'col_1'}, use_global_device_ids=true, to_apply=%region_29.36 | all-reduce | flops 128 | bytes 1024 | tf_op jit(solution)/shard_map/psum | solution.py:50
  329.8 0.7 cholesky.81
  332.5 0.9 convolution_multiply_fusion
  (87 shorter events, 19.5 us)
Async XLA Ops:
  0.6 0.8 copy-start
  49.9 11.4 %all-to-all-start = ((bf16[16,8,1024]{2,1,0:T(8,128)(2,1)}), bf16[16,8,1024]{2,1,0:T(8,128)(2,1)S(1)}, u32[]{:S(2)}, u32[]{:S(2)}) async-start(bf16[16,8,1024]{2,1,0:T(8,128)(2,1)} %broadcast_in_dim.45), calls=%async_computation | async-start | bytes 524288 | tf_op jit(solution)/shard_map/all_to_all | solution.py:20
  70.3 11.5 %all-to-all-start.2 = ((f32[8,8,1024]{2,1,0:T(8,128)}), f32[8,8,1024]{2,1,0:T(8,128)S(1)}, u32[]{:S(2)}, u32[]{:S(2)}) async-start(f32[8,8,1024]{2,1,0:T(8,128)} %copy.60), calls=%async_computation.2 | async-start | bytes 524288 | tf_op jit(solution)/shard_map/all_to_all | solution.py:44
  81.8 69.0 %all-to-all-start.3 = ((f32[16,8,1024]{2,1,0:T(8,128)}), f32[16,8,1024]{2,1,0:T(8,128)S(1)}, u32[]{:S(2)}, u32[]{:S(2)}) async-start(f32[16,8,1024]{2,1,0:T(8,128)} %copy.62), calls=%async_computation.3 | async-start | bytes 1048576 | tf_op jit(solution)/shard_map/all_to_all | solution.py:44
  196.0 11.4 %all-to-all-start.4 = ((bf16[16,8,1024]{2,1,0:T(8,128)(2,1)}), bf16[16,8,1024]{2,1,0:T(8,128)(2,1)S(1)}, u32[]{:S(2)}, u32[]{:S(2)}) async-start(bf16[16,8,1024]{2,1,0:T(8,128)(2,1)} %broadcast_in_dim.47), calls=%async_computation.4 | async-start | bytes 524288 | tf_op jit(solution)/shard_map/all_to_all | solution.py:20
  216.4 11.5 %all-to-all-start.6 = ((f32[8,8,1024]{2,1,0:T(8,128)}), f32[8,8,1024]{2,1,0:T(8,128)S(1)}, u32[]{:S(2)}, u32[]{:S(2)}) async-start(f32[8,8,1024]{2,1,0:T(8,128)} %copy.67), calls=%async_computation.6 | async-start | bytes 524288 | tf_op jit(solution)/shard_map/all_to_all | solution.py:44
  228.0 69.0 %all-to-all-start.7 = ((f32[16,8,1024]{2,1,0:T(8,128)}), f32[16,8,1024]{2,1,0:T(8,128)S(1)}, u32[]{:S(2)}, u32[]{:S(2)}) async-start(f32[16,8,1024]{2,1,0:T(8,128)} %copy.69), calls=%async_computation.7 | async-start | bytes 1048576 | tf_op jit(solution)/shard_map/all_to_all | solution.py:44
  329.8 3.6 %copy-start.1 = (f32[16,16]{1,0:T(8,128)}, f32[16,16]{1,0:T(8,128)S(1)}, u32[]{:S(2)}) copy-start(f32[16,16]{1,0:T(8,128)S(1)} %scatter.19) | copy-start | bytes 3076
where the time goes:
time: 335 us; the launch traced here: 333 us
  starting transfers between devices  134 us (40%)
  blocking collectives  114 us (34%)
  waiting for transfers between devices  40.4 us (12%)
  local copies, waits for them, and re-layouts  23.1 us (7%)
  other arithmetic  12.2 us (4%)
  matrix products  7.58 us (2%)
    all_to_all x4, starting transfers between devices, sent_and_summed(): tiles = lax.all_to_all(split_up(value, dim, length), axis, 0, 0, tiled=True)  127 us
    psum x12, blocking collectives, over_axes(): value = lax.psum(value, axis)  98 us
    all_to_all x4, waiting for transfers between devices, sent_and_summed(): tiles = lax.all_to_all(split_up(value, dim, length), axis, 0, 0, tiled=True)  27.3 us
    all_to_all x2, blocking collectives, sent_to_all(): lax.all_to_all(jnp.broadcast_to(value[None], (length, *value.shape)), axi...  15.9 us
    all_to_all x2, waiting for transfers between devices, sent_to_all(): lax.all_to_all(jnp.broadcast_to(value[None], (length, *value.shape)), axi...  13.1 us
    all_to_all x2, starting transfers between devices, sent_to_all(): lax.all_to_all(jnp.broadcast_to(value[None], (length, *value.shape)), axi...  7.06 us
  transfers between devices with their start and end apart: 6, of which 6 were waited for; matrix products, arithmetic and copies ran while one was open for 2% of the time, Pallas kernels for 0%

commit v1 on v0

v1 whole, which is shorter than its diff:
```python
import functools
import math

import jax
import jax.numpy as jnp
from jax import lax
from jax.experimental import pallas as pl
from jax.experimental.pallas import tpu as pltpu
from jax.sharding import PartitionSpec as P

F32 = jnp.float32
BF16 = jnp.bfloat16
MESH = pl.DeviceIdType.MESH

K = 8
LANES = 128
M = 8
SIDE = 4
NR, NC = 16, 8
RB, CB = NC * M, NR * M
SLOTS = 128
BATCH = 4


def bcast(x):
    return jnp.broadcast_to(x, (K, LANES))


def kernel(
    x_in, blocks, rows_s, cols_s, counts_s, rows_v, cols_v,
    next_out, tri_out,
    bl, xb, yb, xall, yall, picks_r, picks_c, res_d, res_t,
    tot_r, tot_c, in_r, in_c, ykb, qown, wbuf,
    msg, msg2, ar_r, ar_c,
    load_sem, send_sem, recv_sem,
):
    r = lax.axis_index("row")
    c = lax.axis_index("col")
    row_iota = lax.broadcasted_iota(jnp.int32, (K, LANES), 0)
    lane_iota = lax.broadcasted_iota(jnp.int32, (K, LANES), 1)

    row_peers = []
    z0, x0 = r // SIDE, lax.rem(r, SIDE)
    for off in range(1, NR):
        dz, dx = off // SIDE, off % SIDE
        row_peers.append(lax.rem(z0 + dz, SIDE) * SIDE + lax.rem(x0 + dx, SIDE))
    col_peers = []
    y0, p0 = c // 2, lax.rem(c, 2)
    for off in range(1, NC):
        dy, dp = off // 2, off % 2
        col_peers.append(lax.rem(y0 + dy, SIDE) * 2 + lax.rem(p0 + dp, 2))

    barrier = pltpu.get_barrier_semaphore()
    for rr in row_peers:
        pl.semaphore_signal(barrier, inc=1, device_id=(rr, c), device_id_type=MESH)
    for cc in col_peers:
        pl.semaphore_signal(barrier, inc=1, device_id=(r, cc), device_id_type=MESH)

    parts = 4
    step = SLOTS // parts
    loads = [
        pltpu.make_async_copy(
            blocks.at[0, 0, pl.ds(i * step, step)], bl.at[pl.ds(i * step, step)], load_sem.at[i]
        )
        for i in range(parts)
    ]
    for load in loads:
        load.start()

    def send(src, dst, sems, dev):
        pltpu.make_async_remote_copy(
            src_ref=src, dst_ref=dst, send_sem=send_sem.at[sems], recv_sem=recv_sem.at[sems],
            device_id=dev, device_id_type=MESH,
        ).start()

    def wait_bytes(ref, sem):
        pltpu.make_async_copy(ref, ref, sem).wait()

    def gram(a_ref, b_ref, lane0, tile):
        for j in range(K):
            acc = None
            for b in range(M):
                term = a_ref[b] * b_ref[b, pl.ds(j, 1), :]
                acc = term if acc is None else acc + term
            col = jnp.sum(acc, axis=1, keepdims=True)
            tile = jnp.where(lane_iota == lane0 + j, bcast(col), tile)
        return tile

    def reduce_rows_start(n, tile):
        msg[n] = tile
        for rr in row_peers:
            send(msg.at[n], ar_r.at[n, r], 6 * n + 0, (rr, c))

    def reduce_finish(n):
        wait_bytes(ar_r.at[n, pl.ds(0, NR - 1)], recv_sem.at[6 * n + 0])
        ar_r[n, r] = msg[n]
        total = ar_r[n, 0]
        for i in range(1, NR):
            total = total + ar_r[n, i]
        msg2[n] = total
        for cc in col_peers:
            send(msg2.at[n], ar_c.at[n, c], 6 * n + 1, (r, cc))
        wait_bytes(ar_c.at[n, pl.ds(0, NC - 1)], recv_sem.at[6 * n + 1])
        ar_c[n, c] = msg2[n]
        total = ar_c[n, 0]
        for i in range(1, NC):
            total = total + ar_c[n, i]
        return total

    def columns(tile, lane0):
        return [bcast(tile[:, lane0 + j : lane0 + j + 1]) for j in range(K)]

    def factor(gcols):
        g = list(gcols)
        d = [jnp.where(row_iota == m, 1.0, 0.0).astype(F32) for m in range(K)]
        unit = []
        diag = g[0]
        for j in range(K):
            inv = 1.0 / g[j][j : j + 1, :]
            f = jnp.where(row_iota > j, g[j] * inv, 0.0)
            unit.append(f + jnp.where(row_iota == j, 1.0, 0.0))
            if j:
                diag = jnp.where(row_iota == j, g[j], diag)
            for m in range(j + 1, K):
                g[m] = g[m] - f * g[m][j : j + 1, :]
            for m in range(j + 1):
                d[m] = d[m] - f * d[m][j : j + 1, :]
        root = jnp.sqrt(diag)
        rs = 1.0 / root
        inverse = [v * rs for v in d]
        upper = [jnp.where(row_iota <= m, g[m], 0.0) * rs for m in range(K)]
        lower = [unit[j] * root[j : j + 1, :] for j in range(K)]
        return inverse, upper, lower

    def matmul_cols(left, right):
        out = []
        for m in range(K):
            acc = left[0] * right[m][0:1, :]
            for p in range(1, K):
                acc = acc + left[p] * right[m][p : p + 1, :]
            out.append(acc)
        return out

    def apply(cols, ref, i):
        acc = cols[0] * ref[i, pl.ds(0, 1), :]
        for j in range(1, K):
            acc = acc + cols[j] * ref[i, pl.ds(j, 1), :]
        return acc

    def gather_start(src, dst, n):
        for rr in row_peers:
            send(src, dst.at[pl.ds(RB + M * r, M)], 6 * n + 2, (rr, c))
        for cc in col_peers:
            send(src, dst.at[pl.ds(M * c, M)], 6 * n + 3, (r, cc))

    def gather_finish(src, dst, n):
        for b in range(M):
            dst[RB + M * r + b] = src[b]
            dst[M * c + b] = src[b]
        wait_bytes(dst.at[pl.ds(0, (NR - 1) * M)], recv_sem.at[6 * n + 2])
        wait_bytes(dst.at[pl.ds(0, (NC - 1) * M)], recv_sem.at[6 * n + 3])

    zero = jnp.zeros((K, LANES), F32)

    def cat(a, b, axis):
        return jnp.concatenate([a, b], axis=axis)

    def product(vec):
        def body(q, carry):
            base = BATCH * q
            b = [bl[base + i] for i in range(BATCH)]
            tile = cat(cat(b[0], b[1], 0), cat(b[2], b[3], 0), 1)
            xr = [vec[rows_s[r, 0, base + i]] for i in range(BATCH)]
            xc = [vec[RB + cols_s[r, 0, base + i]] for i in range(BATCH)]
            lhs_t = jnp.concatenate(
                [cat(xr[0], zero, 1), cat(zero, xr[1], 1), cat(xr[2], zero, 1), cat(zero, xr[3], 1)],
                axis=0,
            ).astype(BF16)
            lhs_d = jnp.concatenate(
                [cat(xc[0], zero, 1), cat(xc[1], zero, 1), cat(zero, xc[2], 1), cat(zero, xc[3], 1)],
                axis=0,
            ).astype(BF16)
            turned = lax.dot_general(
                lhs_t, tile, (((1,), (0,)), ((), ())), preferred_element_type=F32
            )
            direct = lax.dot_general(
                lhs_d, tile, (((1,), (1,)), ((), ())), preferred_element_type=F32
            )
            for i in range(BATCH):
                ht = i // 2
                hd = i % 2
                res_t[pl.ds(base + i, K, stride=SLOTS), :] = turned[
                    K * i : K * i + K, LANES * ht : LANES * ht + LANES
                ]
                res_d[pl.ds(base + i, K, stride=SLOTS), :] = direct[
                    K * i : K * i + K, LANES * hd : LANES * hd + LANES
                ]
            return carry

        lax.fori_loop(0, SLOTS // BATCH, body, 0, unroll=2)

    def scatter(pick, res, tot, pieces):
        for kk in range(K // 2):
            full = cat(
                res[pl.ds(2 * kk * SLOTS, SLOTS), :], res[pl.ds((2 * kk + 1) * SLOTS, SLOTS), :], 1
            )
            hi = full.astype(BF16)
            lo = (full - hi.astype(F32)).astype(BF16)
            out = jnp.dot(pick[...], cat(hi, lo, 0), preferred_element_type=F32)
            for i in range(pieces):
                for h in range(2):
                    tot[i, 2 * kk + h] = out[M * i : M * i + M, LANES * h : LANES * h + LANES]

    def reduce_scatter(n, out_ref):
        for i, rr in enumerate(row_peers):
            send(tot_c.at[n, rr], in_c.at[n, r], 6 * n + 4, (rr, c))
        for i, cc in enumerate(col_peers):
            send(tot_r.at[n, cc], in_r.at[n, c], 6 * n + 5, (r, cc))
        in_c[n, r] = tot_c[n, r]
        in_r[n, c] = tot_r[n, c]
        wait_bytes(in_c.at[n, pl.ds(0, NR - 1)], recv_sem.at[6 * n + 4])
        wait_bytes(in_r.at[n, pl.ds(0, NC - 1)], recv_sem.at[6 * n + 5])
        for k in range(K):
            total = in_c[n, 0, k]
            for i in range(1, NR):
                total = total + in_c[n, i, k]
            for i in range(NC):
                total = total + in_r[n, i, k]
            ykb[pl.ds(M * k, M), :] = total
        for b in range(M):
            out_ref[b] = ykb[pl.ds(b, K, stride=M), :]

    for b in range(M):
        xb[b] = x_in[:, pl.ds(LANES * b, LANES)]
    start_tile = gram(xb, xb, 0, zero)

    giota = lax.broadcasted_iota(jnp.int32, (1, SLOTS), 1)
    row_ids = rows_v[r]
    col_ids = cols_v[r]
    valid = giota < counts_s[r, c]
    global_row = r * RB + row_ids
    global_col = ((col_ids // M) * NC + c) * M + lax.rem(col_ids, M)
    mirror = jnp.logical_and(valid, global_row != global_col)
    want_r = jnp.where(valid, row_ids, -1)
    want_c = jnp.where(mirror, col_ids, -1)
    one_r = jnp.where(lax.broadcasted_iota(jnp.int32, (RB, SLOTS), 0) == want_r, 1.0, 0.0)
    one_c = jnp.where(lax.broadcasted_iota(jnp.int32, (CB, SLOTS), 0) == want_c, 1.0, 0.0)
    one_r = one_r.astype(BF16)
    one_c = one_c.astype(BF16)
    picks_r[...] = cat(one_r, one_r, 1)
    picks_c[...] = cat(one_c, one_c, 1)

    pl.semaphore_wait(barrier, NR + NC - 2)

    reduce_rows_start(0, start_tile)
    gather_start(xb, xall, 0)
    inverse, _, _ = factor(columns(reduce_finish(0), 0))
    gather_finish(xb, xall, 0)

    def normalise(i, carry):
        for u in range(8):
            t = 8 * i + u
            xall[t] = apply(inverse, xall, t)
        return carry

    lax.fori_loop(0, (RB + CB) // 8, normalise, 0)
    for load in loads:
        load.wait()
    product(xall)
    scatter(picks_r, res_d, tot_r.at[0], NC)
    scatter(picks_c, res_t, tot_c.at[0], NR)
    reduce_scatter(0, yb)

    for b in range(M):
        qown[0, b] = xall[M * c + b]
    tile = gram(yb, qown.at[0], 0, zero)
    tile = gram(yb, yb, K, tile)
    tile = gram(qown.at[0], yb, 2 * K, tile)
    reduce_rows_start(1, tile)
    gather_start(yb, yall, 1)
    total = reduce_finish(1)
    at_cols = columns(total, 0)
    s_cols = columns(total, K)
    a1_cols = columns(total, 2 * K)
    ata = matmul_cols(at_cols, a1_cols)
    inverse, upper1, lower1 = factor([s - t for s, t in zip(s_cols, ata)])
    back = matmul_cols(inverse, at_cols)
    gather_finish(yb, yall, 1)

    def advance(i, carry):
        for u in range(4):
            t = 4 * i + u
            yall[t] = apply(inverse, yall, t) - apply(back, xall, t)
        return carry

    lax.fori_loop(0, (RB + CB) // 4, advance, 0)
    product(yall)
    scatter(picks_r, res_d, tot_r.at[1], NC)
    scatter(picks_c, res_t, tot_c.at[1], NR)
    reduce_scatter(1, wbuf)
    for b in range(M):
        qown[1, b] = yall[M * c + b]
        wbuf[b] = wbuf[b] - apply(upper1, qown.at[0], b)
    tile = gram(wbuf, qown.at[1], 0, zero)
    tile = gram(wbuf, wbuf, K, tile)
    tile = gram(qown.at[1], wbuf, 2 * K, tile)
    reduce_rows_start(2, tile)
    total = reduce_finish(2)
    at_cols = columns(total, 0)
    s_cols = columns(total, K)
    a2_cols = columns(total, 2 * K)
    ata = matmul_cols(at_cols, a2_cols)
    inverse, _, _ = factor([s - t for s, t in zip(s_cols, ata)])
    back = matmul_cols(inverse, at_cols)
    order_root = math.sqrt(NR * NC * M * LANES)
    for b in range(M):
        value = apply(inverse, wbuf, b) - apply(back, qown.at[1], b)
        next_out[:, pl.ds(LANES * b, LANES)] = value * order_root
    top = zero
    low = zero
    for j in range(K):
        top = jnp.where(lane_iota == j, a1_cols[j], top)
        top = jnp.where(lane_iota == K + j, lower1[j], top)
        low = jnp.where(lane_iota == j, upper1[j], low)
        low = jnp.where(lane_iota == K + j, a2_cols[j], low)
    tri_out[pl.ds(0, K), :] = top[:, : 2 * K]
    tri_out[pl.ds(K, K), :] = low[:, : 2 * K]

    for n in range(3):
        wait_bytes(ar_r.at[n, pl.ds(0, NR - 1)], send_sem.at[6 * n + 0])
        wait_bytes(ar_c.at[n, pl.ds(0, NC - 1)], send_sem.at[6 * n + 1])
    for n in range(2):
        wait_bytes(xall.at[pl.ds(0, (NR - 1) * M)], send_sem.at[6 * n + 2])
        wait_bytes(xall.at[pl.ds(0, (NC - 1) * M)], send_sem.at[6 * n + 3])
        wait_bytes(in_c.at[n, pl.ds(0, NR - 1)], send_sem.at[6 * n + 4])
        wait_bytes(in_r.at[n, pl.ds(0, NC - 1)], send_sem.at[6 * n + 5])


def per_device(start_block, blocks, block_rows, block_cols, counts):
    vmem = pl.BlockSpec(memory_space=pltpu.VMEM)
    smem = pl.BlockSpec(memory_space=pltpu.SMEM)
    tile = (K, LANES)
    return pl.pallas_call(
        kernel,
        out_shape=(
            jax.ShapeDtypeStruct((K, M * LANES), F32),
            jax.ShapeDtypeStruct((2 * K, 2 * K), F32),
        ),
        in_specs=[vmem, pl.BlockSpec(memory_space=pl.ANY), smem, smem, smem, vmem, vmem],
        out_specs=(vmem, vmem),
        scratch_shapes=[
            pltpu.VMEM((SLOTS, LANES, LANES), BF16),
            pltpu.VMEM((M, *tile), F32),
            pltpu.VMEM((M, *tile), F32),
            pltpu.VMEM((RB + CB, *tile), F32),
            pltpu.VMEM((RB + CB, *tile), F32),
            pltpu.VMEM((RB, 2 * SLOTS), BF16),
            pltpu.VMEM((CB, 2 * SLOTS), BF16),
            pltpu.VMEM((K * SLOTS, LANES), F32),
            pltpu.VMEM((K * SLOTS, LANES), F32),
            pltpu.VMEM((2, NC, K, M, LANES), F32),
            pltpu.VMEM((2, NR, K, M, LANES), F32),
            pltpu.VMEM((2, NC, K, M, LANES), F32),
            pltpu.VMEM((2, NR, K, M, LANES), F32),
            pltpu.VMEM((K * M, LANES), F32),
            pltpu.VMEM((2, M, *tile), F32),
            pltpu.VMEM((M, *tile), F32),
            pltpu.VMEM((3, *tile), F32),
            pltpu.VMEM((3, *tile), F32),
            pltpu.VMEM((3, NR, *tile), F32),
            pltpu.VMEM((3, NC, *tile), F32),
            pltpu.SemaphoreType.DMA((4,)),
            pltpu.SemaphoreType.DMA((18,)),
            pltpu.SemaphoreType.DMA((18,)),
        ],
        compiler_params=pltpu.CompilerParams(
            collective_id=0, has_side_effects=True, vmem_limit_bytes=48 * 1024 * 1024
        ),
        name="lanczos",
    )(start_block, blocks, block_rows, block_cols, counts, block_rows, block_cols)


def solution(mesh):
    assert mesh.shape["row"] == NR and mesh.shape["col"] == NC
    both = ("row", "col")
    return jax.shard_map(
        per_device,
        mesh=mesh,
        in_specs=(
            P(None, both),
            P("row", "col", None, None, None),
            P(None, "col", None),
            P(None, "col", None),
            P(),
        ),
        out_specs=(P(None, both), P()),
        check_vma=False,
    )
```

time: 335 us -> 74.2 us (0.22)
  starting transfers between devices: 134 us -> 0 us
  blocking collectives: 114 us -> 0 us
  Pallas kernels: 0 us -> 66.9 us
  waiting for transfers between devices: 40.4 us -> 0 us
  local copies, waits for them, and re-layouts: 23.1 us -> 6.31 us
  other arithmetic: 12.2 us -> 0 us
  matrix products: 7.58 us -> 0 us
    all_to_all x6 -> x0, starting transfers between devices: 134 us -> none  [the longest x4 127 us: sent_and_summed(): tiles = lax.all_to_all(split_up(value, dim, length), axis, 0, 0, tiled=True)]
    psum x12 -> x0, blocking collectives: 98 us -> none  [over_axes(): value = lax.psum(value, axis)]
    pallas_call x0 -> x1, Pallas kernels: none -> 66.9 us  [per_device(): pl.pallas_call(kernel, out_shape=(jax.ShapeDtypeStruct((K, M * LANES), F3...]
    all_to_all x6 -> x0, waiting for transfers between devices: 40.4 us -> none  [the longest x4 27.3 us: sent_and_summed(): tiles = lax.all_to_all(split_up(value, dim, length), axis, 0, 0, tiled=True)]
    all_to_all x2 -> x0, blocking collectives: 15.9 us -> none  [sent_to_all(): lax.all_to_all(jnp.broadcast_to(value[None], (length, *value.shape)), axi...]
    another operation x17 -> x0, other arithmetic: 10.7 us -> none
    gather x10 -> x0, local copies, waits for them, and re-layouts: 10.6 us -> none  [the longest x2 5.67 us: visit(): tile_data = jnp.take(stored, slot_ids, axis=0)]
    dot_general x18 -> x0, matrix products: 6.27 us -> none  [the longest x2 1.35 us: visit(): jnp.einsum('gs,kgi->ksi', pick_cols, turned, precision=lax.Precision.HIGH...]
  transfers between devices with their start and end apart: 6 -> 0, of which waited for: 6 -> 0; matrix products, arithmetic and copies ran while one was open for 2% -> 0% of each run, Pallas kernels for 0% -> 0%
where the time goes in v1:
time: 74.2 us; the launch traced here: 73.9 us
  Pallas kernels  66.9 us (90%)
  local copies, waits for them, and re-layouts  6.31 us (9%)
    pallas_call x1, Pallas kernels, per_device(): pl.pallas_call(kernel, out_shape=(jax.ShapeDtypeStruct((K, M * LANES), F3...  66.9 us
    unnamed x11, local copies, waits for them, and re-layouts  6.31 us

profile of v1, /device:TPU:1, one launch (start us, length us, event | category | flops | bytes accessed | tf_op | source)
XLA Modules:
  0.0 73.9 jit_solution(10089181893415163979)
XLA Ops:
  0.6 0.8 %copy.7.counts_s = s32[16,8]{1,0:T(8,128)S(1)} copy(s32[16,8]{0,1:T(8,128)} %param.9) | data formatting | bytes 1024 | tf_op args[4]
  1.4 0.0 copy-start
  1.4 2.2 %copy-done = bf16[1,1,128,128,128]{4,3,2,1,0:T(8,128)(2,1)S(1)} copy-done((bf16[1,1,128,128,128]{4,3,2,1,0:T(8,128)(2,1)S(1)}, bf16[1,1,128,128,128]{4,3,2,1,0:T(8,128)(2,1)}, u32[]{:S(2)}) %copy-start) | copy-done | bytes 4194328
  3.6 0.0 copy-start.1
  3.6 0.8 %copy-done.1 = f32[8,1024]{1,0:T(8,128)S(1)} copy-done((f32[8,1024]{1,0:T(8,128)S(1)}, f32[8,1024]{1,0:T(8,128)}, u32[]{:S(2)}) %copy-start.1) | copy-done | bytes 32792
  4.3 0.0 copy-start.2
  4.3 0.7 copy-done.2
  5.0 0.0 copy-start.3
  5.0 0.7 copy-done.3
  5.7 66.9 %lanczos.1 = (f32[8,1024]{1,0:T(8,128)S(1)}, f32[16,16]{1,0:T(8,128)S(1)}) custom-call(f32[8,1024]{1,0:T(8,128)S(1)} %copy-done.1, bf16[1,1,128,128,128]{4,3,2,1,0:T(8,128)(2,1)S(1)} %copy-done, s32[16,1,128]{2,1,0:T(1,128)S(1)} %copy-done.2, s32[16,1,128]{2,1,0:T(1,128)S(1)} %copy-done.3, s32[16,8]{1,0:T(8,128)S(1)} %copy.7.counts_s, ...), custom_call_target="tpu_custom_call" | custom-call | tf_op jit(solution)/shard_map/lanczos/pallas_call | solution.py:343
  72.7 0.6 copy.10
  73.3 0.6 copy.11
Async XLA Ops:
  1.4 2.2 %copy-start = (bf16[1,1,128,128,128]{4,3,2,1,0:T(8,128)(2,1)S(1)}, bf16[1,1,128,128,128]{4,3,2,1,0:T(8,128)(2,1)}, u32[]{:S(2)}) copy-start(bf16[1,1,128,128,128]{4,3,2,1,0:T(8,128)(2,1)} %blocks.1) | copy-start | bytes 12582916
  3.6 0.8 %copy-start.1 = (f32[8,1024]{1,0:T(8,128)S(1)}, f32[8,1024]{1,0:T(8,128)}, u32[]{:S(2)}) copy-start(f32[8,1024]{1,0:T(8,128)} %x_in.1) | copy-start | bytes 98308
  4.3 0.7 copy-start.2
  5.0 0.7 copy-start.3

commit v2 on v1

v2 whole, which is shorter than its diff:
```python
import functools
import math

import jax
import jax.numpy as jnp
from jax import lax
from jax.experimental import pallas as pl
from jax.experimental.pallas import tpu as pltpu
from jax.sharding import PartitionSpec as P

F32 = jnp.float32
BF16 = jnp.bfloat16
MESH = pl.DeviceIdType.MESH

K = 8
LANES = 128
M = 8
SIDE = 4
NR, NC = 16, 8
RB, CB = NC * M, NR * M
SLOTS = 128
BATCH = 4
UNROLL = 16
SUM_C = BF16
SUM_R = BF16


def bcast(x):
    return jnp.broadcast_to(x, (K, LANES))


def kernel(
    x_hbm, blocks, rows_hbm, cols_hbm, counts_hbm,
    next_out, tri_out,
    bl, x_in, rows_s, cols_s, counts_s, rows_v, cols_v, xb, yb, xr, xc, yr, yc, picks_r, picks_c, res_d, res_t,
    tot_r, tot_c, in_r, in_c, ykb, qown, wbuf, msg, ar,
    load_sem, send_sem, recv_sem,
):
    r = lax.axis_index("row")
    c = lax.axis_index("col")
    row_iota = lax.broadcasted_iota(jnp.int32, (K, LANES), 0)
    lane_iota = lax.broadcasted_iota(jnp.int32, (K, LANES), 1)

    row_peers = []
    z0, x0 = r // SIDE, lax.rem(r, SIDE)
    for off in range(1, NR):
        dz, dx = off // SIDE, off % SIDE
        row_peers.append(lax.rem(z0 + dz, SIDE) * SIDE + lax.rem(x0 + dx, SIDE))
    col_peers = []
    y0, p0 = c // 2, lax.rem(c, 2)
    for off in range(1, NC):
        dy, dp = off // 2, off % 2
        col_peers.append(lax.rem(y0 + dy, SIDE) * 2 + lax.rem(p0 + dp, 2))

    others = [(rr, cc) for cc in [c] + col_peers for rr in [r] + row_peers][1:]
    others = others[::-1]

    barrier = pltpu.get_barrier_semaphore()
    for dev in others:
        pl.semaphore_signal(barrier, inc=1, device_id=dev, device_id_type=MESH)

    parts = 4
    step = SLOTS // parts
    loads = [
        pltpu.make_async_copy(
            blocks.at[0, 0, pl.ds(i * step, step)], bl.at[pl.ds(i * step, step)], load_sem.at[i]
        )
        for i in range(parts)
    ]
    small = [
        pltpu.make_async_copy(src, dst, load_sem.at[parts + i])
        for i, (src, dst) in enumerate(
            [
                (x_hbm, x_in),
                (rows_hbm.at[r], rows_s),
                (cols_hbm.at[r], cols_s),
                (counts_hbm, counts_s),
                (rows_hbm.at[r], rows_v),
                (cols_hbm.at[r], cols_v),
            ]
        )
    ]
    for load in small + loads:
        load.start()

    def send(src, dst, sems, dev):
        pltpu.make_async_remote_copy(
            src_ref=src, dst_ref=dst, send_sem=send_sem.at[sems], recv_sem=recv_sem.at[sems],
            device_id=dev, device_id_type=MESH,
        ).start()

    def wait_bytes(ref, sem):
        pltpu.make_async_copy(ref, ref, sem).wait()

    def gram(a_ref, b_ref, lane0, tile):
        for j in range(K):
            acc = None
            for b in range(M):
                term = a_ref[b] * b_ref[b, pl.ds(j, 1), :]
                acc = term if acc is None else acc + term
            col = jnp.sum(acc, axis=1, keepdims=True)
            tile = jnp.where(lane_iota == 2 * K * row_iota + (lane0 + j), bcast(col), tile)
        return tile

    def reduce_start(n, tile):
        msg[n] = jnp.sum(tile, axis=0, keepdims=True)
        for dev in others:
            send(msg.at[n], ar.at[n, r * NC + c], 6 * n, dev)

    def reduce_finish(n):
        wait_bytes(ar.at[n, pl.ds(0, NR * NC - 1)], recv_sem.at[6 * n])
        ar[n, r * NC + c] = msg[n]
        sums = [ar[n, i] for i in range(8)]
        for i in range(8, NR * NC):
            sums[i % 8] = sums[i % 8] + ar[n, i]
        while len(sums) > 1:
            sums = [p + q for p, q in zip(sums[::2], sums[1::2])]
        return bcast(sums[0])

    def picked(total, lanes):
        return bcast(jnp.sum(jnp.where(lane_iota == lanes, total, 0.0), axis=1, keepdims=True))

    def columns(total, lane0):
        return [picked(total, 2 * K * row_iota + (lane0 + j)) for j in range(K)]

    def rows_of(total):
        return [picked(total, row_iota + 2 * K * j) for j in range(K)]

    def factor(gcols):
        g = list(gcols)
        d = [jnp.where(row_iota == m, 1.0, 0.0).astype(F32) for m in range(K)]
        unit = []
        diag = g[0]
        for j in range(K):
            inv = 1.0 / g[j][j : j + 1, :]
            f = jnp.where(row_iota > j, g[j] * inv, 0.0)
            unit.append(f + jnp.where(row_iota == j, 1.0, 0.0))
            if j:
                diag = jnp.where(row_iota == j, g[j], diag)
            for m in range(j + 1, K):
                g[m] = g[m] - f * g[m][j : j + 1, :]
            for m in range(j + 1):
                d[m] = d[m] - f * d[m][j : j + 1, :]
        root = jnp.sqrt(diag)
        rs = 1.0 / root
        inverse = [v * rs for v in d]
        upper = [jnp.where(row_iota <= m, g[m], 0.0) * rs for m in range(K)]
        lower = [unit[j] * root[j : j + 1, :] for j in range(K)]
        return inverse, upper, lower

    def matmul_cols(left, right):
        out = []
        for m in range(K):
            acc = left[0] * right[m][0:1, :]
            for p in range(1, K):
                acc = acc + left[p] * right[m][p : p + 1, :]
            out.append(acc)
        return out

    def apply(cols, ref, i):
        acc = cols[0] * ref[i, pl.ds(0, 1), :]
        for j in range(1, K):
            acc = acc + cols[j] * ref[i, pl.ds(j, 1), :]
        return acc

    def gather_start(src, seg_r, seg_c, n):
        for cc in col_peers:
            send(src, seg_r.at[pl.ds(M * c, M)], 6 * n + 3, (r, cc))
        for rr in row_peers:
            send(src, seg_c.at[pl.ds(M * r, M)], 6 * n + 2, (rr, c))
        for b in range(M):
            seg_c[M * r + b] = src[b]
            seg_r[M * c + b] = src[b]

    def gather_wait_col(seg_r, n):
        wait_bytes(seg_r.at[pl.ds(0, (NC - 1) * M)], recv_sem.at[6 * n + 3])

    def gather_wait_row(seg_c, n):
        wait_bytes(seg_c.at[pl.ds(0, (NR - 1) * M)], recv_sem.at[6 * n + 2])

    zero = jnp.zeros((K, LANES), F32)

    def cat(a, b, axis):
        return jnp.concatenate([a, b], axis=axis)

    def product(vec, ids, turn, res):
        def body(q, carry):
            base = BATCH * q
            b = [bl[base + i] for i in range(BATCH)]
            tile = cat(cat(b[0], b[1], 0), cat(b[2], b[3], 0), 1)
            x = [vec[ids[0, base + i]] for i in range(BATCH)]
            depth = [i % 2 if turn else i // 2 for i in range(BATCH)]
            width = [i // 2 if turn else i % 2 for i in range(BATCH)]
            lhs = jnp.concatenate(
                [cat(zero, x[i], 1) if depth[i] else cat(x[i], zero, 1) for i in range(BATCH)],
                axis=0,
            ).astype(BF16)
            out = lax.dot_general(
                lhs, tile, (((1,), (0 if turn else 1,)), ((), ())), preferred_element_type=F32
            )
            for i in range(BATCH):
                res[pl.ds(base + i, K, stride=SLOTS), :] = out[
                    K * i : K * i + K, LANES * width[i] : LANES * width[i] + LANES
                ]
            return carry

        lax.fori_loop(0, SLOTS // BATCH, body, 0, unroll=UNROLL)

    def scatter(pick, res, put):
        for kk in range(K // 2):
            full = cat(
                res[pl.ds(2 * kk * SLOTS, SLOTS), :], res[pl.ds((2 * kk + 1) * SLOTS, SLOTS), :], 1
            )
            hi = full.astype(BF16)
            lo = (full - hi.astype(F32)).astype(BF16)
            put(kk, jnp.dot(pick[...], cat(hi, lo, 0), preferred_element_type=F32))

    def exchange_cols(n):
        def put(kk, out):
            for i in range(NR):
                rows = out[M * i : M * i + M]
                tot_c[n, i, kk] = cat(rows[:, :LANES], rows[:, LANES:], 0).astype(tot_c.dtype)

        scatter(picks_c, res_t, put)
        for rr in row_peers:
            send(tot_c.at[n, rr], in_c.at[n, r], 6 * n + 4, (rr, c))
        in_c[n, r] = tot_c[n, r]

    def exchange_rows(n):
        def put(kk, out):
            for i in range(NC):
                rows = out[M * i : M * i + M]
                tot_r[n, i, kk] = cat(rows[:, :LANES], rows[:, LANES:], 0).astype(tot_r.dtype)

        scatter(picks_r, res_d, put)
        for cc in col_peers:
            send(tot_r.at[n, cc], in_r.at[n, c], 6 * n + 5, (r, cc))
        in_r[n, c] = tot_r[n, c]

    def exchange_finish(n, out_ref):
        wait_bytes(in_r.at[n, pl.ds(0, NC - 1)], recv_sem.at[6 * n + 5])
        for kk in range(K // 2):
            total = in_r[n, 0, kk].astype(F32)
            for i in range(1, NC):
                total = total + in_r[n, i, kk].astype(F32)
            ykb[pl.ds(2 * M * kk, 2 * M), :] = total
        wait_bytes(in_c.at[n, pl.ds(0, NR - 1)], recv_sem.at[6 * n + 4])
        for kk in range(K // 2):
            total = ykb[pl.ds(2 * M * kk, 2 * M), :]
            for i in range(NR):
                total = total + in_c[n, i, kk].astype(F32)
            ykb[pl.ds(2 * M * kk, 2 * M), :] = total
        for b in range(M):
            out_ref[b] = ykb[pl.ds(b, K, stride=M), :]

    def sweep(count, step, update):
        def body(i, carry):
            for u in range(step):
                update(step * i + u)
            return carry

        lax.fori_loop(0, count // step, body, 0)

    for load in small:
        load.wait()
    for b in range(M):
        xb[b] = x_in[:, pl.ds(LANES * b, LANES)]
    start_tile = gram(xb, xb, 0, zero)

    giota = lax.broadcasted_iota(jnp.int32, (1, SLOTS), 1)
    row_ids = rows_v[...]
    col_ids = cols_v[...]
    valid = giota < counts_s[c, r]
    global_row = r * RB + row_ids
    global_col = ((col_ids // M) * NC + c) * M + lax.rem(col_ids, M)
    mirror = jnp.logical_and(valid, global_row != global_col)
    want_r = jnp.where(valid, row_ids, -1)
    want_c = jnp.where(mirror, col_ids, -1)
    one_r = jnp.where(lax.broadcasted_iota(jnp.int32, (RB, SLOTS), 0) == want_r, 1.0, 0.0)
    one_c = jnp.where(lax.broadcasted_iota(jnp.int32, (CB, SLOTS), 0) == want_c, 1.0, 0.0)
    one_r = one_r.astype(BF16)
    one_c = one_c.astype(BF16)
    picks_r[...] = cat(one_r, one_r, 1)
    picks_c[...] = cat(one_c, one_c, 1)

    pl.semaphore_wait(barrier, NR * NC - 1)

    reduce_start(0, start_tile)
    gather_start(xb, xr, xc, 0)
    inverse, _, _ = factor(columns(reduce_finish(0), 0))

    def normalise(seg, t):
        seg[t] = apply(inverse, seg, t)

    gather_wait_col(xr, 0)
    sweep(RB, 8, functools.partial(normalise, xr))
    for load in loads:
        load.wait()
    product(xr, rows_s, True, res_t)
    exchange_cols(0)
    gather_wait_row(xc, 0)
    sweep(CB, 8, functools.partial(normalise, xc))
    product(xc, cols_s, False, res_d)
    exchange_rows(0)
    for b in range(M):
        qown[0, b] = xr[M * c + b]
    exchange_finish(0, yb)

    tile = gram(yb, qown.at[0], 0, zero)
    tile = gram(yb, yb, K, tile)
    reduce_start(1, tile)
    gather_start(yb, yr, yc, 1)
    total = reduce_finish(1)
    at_cols = columns(total, 0)
    s_cols = columns(total, K)
    a1_cols = rows_of(total)
    ata = matmul_cols(at_cols, a1_cols)
    inverse, upper1, lower1 = factor([s - t for s, t in zip(s_cols, ata)])
    back = matmul_cols(inverse, at_cols)

    def advance(seg, old, t):
        seg[t] = apply(inverse, seg, t) - apply(back, old, t)

    gather_wait_col(yr, 1)
    sweep(RB, 4, functools.partial(advance, yr, xr))
    product(yr, rows_s, True, res_t)
    exchange_cols(1)
    gather_wait_row(yc, 1)
    sweep(CB, 4, functools.partial(advance, yc, xc))
    product(yc, cols_s, False, res_d)
    exchange_rows(1)
    for b in range(M):
        qown[1, b] = yr[M * c + b]
    top = zero
    for j in range(K):
        top = jnp.where(lane_iota == j, a1_cols[j], top)
        top = jnp.where(lane_iota == K + j, lower1[j], top)
    tri_out[pl.ds(0, K), :] = top[:, : 2 * K]
    exchange_finish(1, wbuf)
    for b in range(M):
        wbuf[b] = wbuf[b] - apply(upper1, qown.at[0], b)
    tile = gram(wbuf, qown.at[1], 0, zero)
    tile = gram(wbuf, wbuf, K, tile)
    reduce_start(2, tile)

    for n in range(2):
        wait_bytes(ar.at[n, pl.ds(0, NR * NC - 1)], send_sem.at[6 * n])
        wait_bytes(xc.at[pl.ds(0, (NR - 1) * M)], send_sem.at[6 * n + 2])
        wait_bytes(xr.at[pl.ds(0, (NC - 1) * M)], send_sem.at[6 * n + 3])
        wait_bytes(in_c.at[n, pl.ds(0, NR - 1)], send_sem.at[6 * n + 4])
        wait_bytes(in_r.at[n, pl.ds(0, NC - 1)], send_sem.at[6 * n + 5])

    total = reduce_finish(2)
    at_cols = columns(total, 0)
    s_cols = columns(total, K)
    a2_cols = rows_of(total)
    ata = matmul_cols(at_cols, a2_cols)
    inverse, _, _ = factor([s - t for s, t in zip(s_cols, ata)])
    back = matmul_cols(inverse, at_cols)
    order_root = math.sqrt(NR * NC * M * LANES)
    for b in range(M):
        value = apply(inverse, wbuf, b) - apply(back, qown.at[1], b)
        next_out[:, pl.ds(LANES * b, LANES)] = value * order_root
    low = zero
    for j in range(K):
        low = jnp.where(lane_iota == j, upper1[j], low)
        low = jnp.where(lane_iota == K + j, a2_cols[j], low)
    tri_out[pl.ds(K, K), :] = low[:, : 2 * K]
    wait_bytes(ar.at[2, pl.ds(0, NR * NC - 1)], send_sem.at[12])


def per_device(start_block, blocks, block_rows, block_cols, counts):
    vmem = pl.BlockSpec(memory_space=pltpu.VMEM)
    hbm = pl.BlockSpec(memory_space=pltpu.HBM)
    tile = (K, LANES)
    return pl.pallas_call(
        kernel,
        out_shape=(
            jax.ShapeDtypeStruct((K, M * LANES), F32),
            jax.ShapeDtypeStruct((2 * K, 2 * K), F32),
        ),
        in_specs=[hbm] * 5,
        out_specs=(vmem, vmem),
        scratch_shapes=[
            pltpu.VMEM((SLOTS, LANES, LANES), BF16),
            pltpu.VMEM((K, M * LANES), F32),
            pltpu.SMEM((1, SLOTS), jnp.int32),
            pltpu.SMEM((1, SLOTS), jnp.int32),
            pltpu.SMEM((NC, NR), jnp.int32),
            pltpu.VMEM((1, SLOTS), jnp.int32),
            pltpu.VMEM((1, SLOTS), jnp.int32),
            pltpu.VMEM((M, *tile), F32),
            pltpu.VMEM((M, *tile), F32),
            pltpu.VMEM((RB, *tile), F32),
            pltpu.VMEM((CB, *tile), F32),
            pltpu.VMEM((RB, *tile), F32),
            pltpu.VMEM((CB, *tile), F32),
            pltpu.VMEM((RB, 2 * SLOTS), BF16),
            pltpu.VMEM((CB, 2 * SLOTS), BF16),
            pltpu.VMEM((K * SLOTS, LANES), F32),
            pltpu.VMEM((K * SLOTS, LANES), F32),
            pltpu.VMEM((2, NC, K // 2, 2 * M, LANES), SUM_R),
            pltpu.VMEM((2, NR, K // 2, 2 * M, LANES), SUM_C),
            pltpu.VMEM((2, NC, K // 2, 2 * M, LANES), SUM_R),
            pltpu.VMEM((2, NR, K // 2, 2 * M, LANES), SUM_C),
            pltpu.VMEM((K * M, LANES), F32),
            pltpu.VMEM((2, M, *tile), F32),
            pltpu.VMEM((M, *tile), F32),
            pltpu.VMEM((3, 1, LANES), F32),
            pltpu.VMEM((3, NR * NC, 1, LANES), F32),
            pltpu.SemaphoreType.DMA((10,)),
            pltpu.SemaphoreType.DMA((18,)),
            pltpu.SemaphoreType.DMA((18,)),
        ],
        compiler_params=pltpu.CompilerParams(
            collective_id=0, has_side_effects=True, vmem_limit_bytes=67043328
        ),
        name="lanczos",
    )(start_block, blocks, block_rows, block_cols, counts.T)


def solution(mesh):
    assert mesh.shape["row"] == NR and mesh.shape["col"] == NC
    both = ("row", "col")
    return jax.shard_map(
        per_device,
        mesh=mesh,
        in_specs=(
            P(None, both),
            P("row", "col", None, None, None),
            P(None, "col", None),
            P(None, "col", None),
            P(),
        ),
        out_specs=(P(None, both), P()),
        check_vma=False,
    )
```

time: 74.2 us -> 55.3 us (0.75)
  Pallas kernels: 66.9 us -> 51.8 us
  local copies, waits for them, and re-layouts: 6.31 us -> 2.67 us
    pallas_call x1, Pallas kernels: 66.9 us -> 51.8 us  [per_device(): pl.pallas_call(kernel, out_shape=(jax.ShapeDtypeStruct((K, M * LANES), F3...]
    unnamed x11 -> x2, local copies, waits for them, and re-layouts: 6.31 us -> 2.67 us
where the time goes in v2:
time: 55.3 us; the launch traced here: 55.1 us
  Pallas kernels  51.8 us (94%)
  local copies, waits for them, and re-layouts  2.67 us (5%)
  between operations  0.64 us (1%)
    pallas_call x1, Pallas kernels, per_device(): pl.pallas_call(kernel, out_shape=(jax.ShapeDtypeStruct((K, M * LANES), F3...  51.8 us
    unnamed x2, local copies, waits for them, and re-layouts  2.67 us

profile of v2, /device:TPU:1, one launch (start us, length us, event | category | flops | bytes accessed | tf_op | source)
XLA Modules:
  0.0 55.1 jit_solution(13899096218655642279)
XLA Ops:
  0.6 51.8 %lanczos.1 = (f32[8,1024]{1,0:T(8,128)}, f32[16,16]{1,0:T(8,128)}) custom-call(f32[8,1024]{1,0:T(8,128)} %x_hbm.1, bf16[1,1,128,128,128]{4,3,2,1,0:T(8,128)(2,1)} %blocks.1, s32[16,1,128]{2,1,0:T(1,128)} %rows_hbm.1, s32[16,1,128]{2,1,0:T(1,128)} %cols_hbm.1, s32[8,16]{1,0:T(8,128)} %bitcast.1), custom_call_target="tpu_custom_call" | custom-call | tf_op jit(solution)/shard_map/lanczos/pallas_call | solution.py:376
  52.4 1.4 %copy.9 = f32[8,1024]{1,0:T(8,128)} copy(f32[8,1024]{1,0:T(8,128)} %get-tuple-element.4) | data formatting | bytes 65536
  53.8 1.3 %copy.10 = f32[16,16]{1,0:T(8,128)} copy(f32[16,16]{1,0:T(8,128)} %get-tuple-element.5) | data formatting | bytes 2048

commit v3 on v2

--- a/solution.py
+++ b/solution.py
@@ -32,8 +32,8 @@
 def kernel(
     x_hbm, blocks, rows_hbm, cols_hbm, counts_hbm,
     next_out, tri_out,
-    bl, x_in, rows_s, cols_s, counts_s, rows_v, cols_v, xb, yb, xr, xc, yr, yc, picks_r, picks_c, res_d, res_t,
-    tot_r, tot_c, in_r, in_c, ykb, qown, wbuf, msg, ar,
+    bl, blt, x_in, rows_s, cols_s, counts_s, rows_v, cols_v, xb, yb, xr, xc, yr, yc, picks_r, picks_c, res_d, res_t,
+    tot_r, tot_c, in_r, in_c, ykb, qown, wbuf, msg, ar, first, first_r, first_c,
     load_sem, send_sem, recv_sem,
 ):
     r = lax.axis_index("row")
@@ -41,23 +41,33 @@
     row_iota = lax.broadcasted_iota(jnp.int32, (K, LANES), 0)
     lane_iota = lax.broadcasted_iota(jnp.int32, (K, LANES), 1)
 
-    row_peers = []
+    def far(off):
+        return -sum(min(d, SIDE - d) for d in off[:3]), off
+
     z0, x0 = r // SIDE, lax.rem(r, SIDE)
-    for off in range(1, NR):
-        dz, dx = off // SIDE, off % SIDE
-        row_peers.append(lax.rem(z0 + dz, SIDE) * SIDE + lax.rem(x0 + dx, SIDE))
-    col_peers = []
     y0, p0 = c // 2, lax.rem(c, 2)
-    for off in range(1, NC):
-        dy, dp = off // 2, off % 2
-        col_peers.append(lax.rem(y0 + dy, SIDE) * 2 + lax.rem(p0 + dp, 2))
-
-    others = [(rr, cc) for cc in [c] + col_peers for rr in [r] + row_peers][1:]
-    others = others[::-1]
+    row_at = {
+        (dz, dx): lax.rem(z0 + dz, SIDE) * SIDE + lax.rem(x0 + dx, SIDE) if dz + dx else r
+        for dz in range(SIDE)
+        for dx in range(SIDE)
+    }
+    col_at = {
+        (dy, dp): lax.rem(y0 + dy, SIDE) * 2 + lax.rem(p0 + dp, 2) if dy + dp else c
+        for dy in range(SIDE)
+        for dp in range(2)
+    }
+    offsets = sorted(
+        ((dz, dx, dy, dp) for dz, dx in row_at for dy, dp in col_at if dz + dx + dy + dp), key=far
+    )
+    others = [(row_at[o[:2]], col_at[o[2:]]) for o in offsets]
+    row_peers = [row_at[o[:2]] for o in offsets if o[2:] == (0, 0)]
+    col_peers = [col_at[o[2:]] for o in offsets if o[:2] == (0, 0)]
 
     barrier = pltpu.get_barrier_semaphore()
-    for dev in others:
-        pl.semaphore_signal(barrier, inc=1, device_id=dev, device_id_type=MESH)
+    for rr in row_peers:
+        pl.semaphore_signal(barrier, inc=1, device_id=(rr, c), device_id_type=MESH)
+    for cc in col_peers:
+        pl.semaphore_signal(barrier, inc=1, device_id=(r, cc), device_id_type=MESH)
 
     parts = 4
     step = SLOTS // parts
@@ -102,6 +112,26 @@
             tile = jnp.where(lane_iota == 2 * K * row_iota + (lane0 + j), bcast(col), tile)
         return tile
 
+    def tree(terms):
+        while len(terms) > 1:
+            terms = [p + q for p, q in zip(terms[::2], terms[1::2])]
+        return terms[0]
+
+    def first_reduce_start(tile):
+        first[0] = jnp.sum(tile, axis=0, keepdims=True)
+        for rr in row_peers:
+            send(first.at[0], first_r.at[r], 18, (rr, c))
+
+    def first_reduce_finish():
+        wait_bytes(first_r.at[pl.ds(0, NR - 1)], recv_sem.at[18])
+        first_r[r] = first[0]
+        first[1] = tree([first_r[i] for i in range(NR)])
+        for cc in col_peers:
+            send(first.at[1], first_c.at[c], 19, (r, cc))
+        wait_bytes(first_c.at[pl.ds(0, NC - 1)], recv_sem.at[19])
+        first_c[c] = first[1]
+        return bcast(tree([first_c[i] for i in range(NC)]))
+
     def reduce_start(n, tile):
         msg[n] = jnp.sum(tile, axis=0, keepdims=True)
         for dev in others:
@@ -113,9 +143,7 @@
         sums = [ar[n, i] for i in range(8)]
         for i in range(8, NR * NC):
             sums[i % 8] = sums[i % 8] + ar[n, i]
-        while len(sums) > 1:
-            sums = [p + q for p, q in zip(sums[::2], sums[1::2])]
-        return bcast(sums[0])
+        return bcast(tree(sums))
 
     def picked(total, lanes):
         return bcast(jnp.sum(jnp.where(lane_iota == lanes, total, 0.0), axis=1, keepdims=True))
@@ -183,25 +211,19 @@
     def cat(a, b, axis):
         return jnp.concatenate([a, b], axis=axis)
 
-    def product(vec, ids, turn, res):
+    def product(vec, ids, mats, res):
         def body(q, carry):
             base = BATCH * q
-            b = [bl[base + i] for i in range(BATCH)]
+            b = [mats[base + i] for i in range(BATCH)]
             tile = cat(cat(b[0], b[1], 0), cat(b[2], b[3], 0), 1)
             x = [vec[ids[0, base + i]] for i in range(BATCH)]
-            depth = [i % 2 if turn else i // 2 for i in range(BATCH)]
-            width = [i // 2 if turn else i % 2 for i in range(BATCH)]
             lhs = jnp.concatenate(
-                [cat(zero, x[i], 1) if depth[i] else cat(x[i], zero, 1) for i in range(BATCH)],
-                axis=0,
+                [cat(zero, x[i], 1) if i % 2 else cat(x[i], zero, 1) for i in range(BATCH)], axis=0
             ).astype(BF16)
-            out = lax.dot_general(
-                lhs, tile, (((1,), (0 if turn else 1,)), ((), ())), preferred_element_type=F32
-            )
+            out = jnp.dot(lhs, tile, preferred_element_type=F32)
             for i in range(BATCH):
-                res[pl.ds(base + i, K, stride=SLOTS), :] = out[
-                    K * i : K * i + K, LANES * width[i] : LANES * width[i] + LANES
-                ]
+                half = LANES * (i // 2)
+                res[pl.ds(base + i, K, stride=SLOTS), :] = out[K * i : K * i + K, half : half + LANES]
             return carry
 
         lax.fori_loop(0, SLOTS // BATCH, body, 0, unroll=UNROLL)
@@ -283,24 +305,31 @@
     picks_r[...] = cat(one_r, one_r, 1)
     picks_c[...] = cat(one_c, one_c, 1)
 
-    pl.semaphore_wait(barrier, NR * NC - 1)
-
-    reduce_start(0, start_tile)
+    pl.semaphore_wait(barrier, NR + NC - 2)
+
+    first_reduce_start(start_tile)
     gather_start(xb, xr, xc, 0)
-    inverse, _, _ = factor(columns(reduce_finish(0), 0))
+    for load in loads:
+        load.wait()
+
+    def turn(i, carry):
+        for u in range(8):
+            blt[8 * i + u] = bl[8 * i + u].T
+        return carry
+
+    lax.fori_loop(0, SLOTS // 8, turn, 0)
+    inverse, _, _ = factor(columns(first_reduce_finish(), 0))
 
     def normalise(seg, t):
         seg[t] = apply(inverse, seg, t)
 
     gather_wait_col(xr, 0)
     sweep(RB, 8, functools.partial(normalise, xr))
-    for load in loads:
-        load.wait()
-    product(xr, rows_s, True, res_t)
+    product(xr, rows_s, bl, res_t)
     exchange_cols(0)
     gather_wait_row(xc, 0)
     sweep(CB, 8, functools.partial(normalise, xc))
-    product(xc, cols_s, False, res_d)
+    product(xc, cols_s, blt, res_d)
     exchange_rows(0)
     for b in range(M):
         qown[0, b] = xr[M * c + b]
@@ -323,11 +352,11 @@
 
     gather_wait_col(yr, 1)
     sweep(RB, 4, functools.partial(advance, yr, xr))
-    product(yr, rows_s, True, res_t)
+    product(yr, rows_s, bl, res_t)
     exchange_cols(1)
     gather_wait_row(yc, 1)
     sweep(CB, 4, functools.partial(advance, yc, xc))
-    product(yc, cols_s, False, res_d)
+    product(yc, cols_s, blt, res_d)
     exchange_rows(1)
     for b in range(M):
         qown[1, b] = yr[M * c + b]
@@ -343,8 +372,10 @@
     tile = gram(wbuf, wbuf, K, tile)
     reduce_start(2, tile)
 
+    wait_bytes(first_r.at[pl.ds(0, NR - 1)], send_sem.at[18])
+    wait_bytes(first_c.at[pl.ds(0, NC - 1)], send_sem.at[19])
+    wait_bytes(ar.at[1, pl.ds(0, NR * NC - 1)], send_sem.at[6])
     for n in range(2):
-        wait_bytes(ar.at[n, pl.ds(0, NR * NC - 1)], send_sem.at[6 * n])
         wait_bytes(xc.at[pl.ds(0, (NR - 1) * M)], send_sem.at[6 * n + 2])
         wait_bytes(xr.at[pl.ds(0, (NC - 1) * M)], send_sem.at[6 * n + 3])
         wait_bytes(in_c.at[n, pl.ds(0, NR - 1)], send_sem.at[6 * n + 4])
@@ -370,6 +401,7 @@
 
 
 def per_device(start_block, blocks, block_rows, block_cols, counts):
+    args = (start_block, blocks, block_rows, block_cols, counts.T)
     vmem = pl.BlockSpec(memory_space=pltpu.VMEM)
     hbm = pl.BlockSpec(memory_space=pltpu.HBM)
     tile = (K, LANES)
@@ -382,6 +414,7 @@
         in_specs=[hbm] * 5,
         out_specs=(vmem, vmem),
         scratch_shapes=[
+            pltpu.VMEM((SLOTS, LANES, LANES), BF16),
             pltpu.VMEM((SLOTS, LANES, LANES), BF16),
             pltpu.VMEM((K, M * LANES), F32),
             pltpu.SMEM((1, SLOTS), jnp.int32),
@@ -408,15 +441,18 @@
             pltpu.VMEM((M, *tile), F32),
             pltpu.VMEM((3, 1, LANES), F32),
             pltpu.VMEM((3, NR * NC, 1, LANES), F32),
+            pltpu.VMEM((2, 1, LANES), F32),
+            pltpu.VMEM((NR, 1, LANES), F32),
+            pltpu.VMEM((NC, 1, LANES), F32),
             pltpu.SemaphoreType.DMA((10,)),
-            pltpu.SemaphoreType.DMA((18,)),
-            pltpu.SemaphoreType.DMA((18,)),
+            pltpu.SemaphoreType.DMA((20,)),
+            pltpu.SemaphoreType.DMA((20,)),
         ],
         compiler_params=pltpu.CompilerParams(
-            collective_id=0, has_side_effects=True, vmem_limit_bytes=67043328
+            collective_id=0, has_side_effects=True, vmem_limit_bytes=48 * 1024 * 1024
         ),
         name="lanczos",
-    )(start_block, blocks, block_rows, block_cols, counts.T)
+    )(*[pltpu.with_memory_space_constraint(v, pltpu.HBM) for v in args])
 
 
 def solution(mesh):

time: 55.3 us -> 49.3 us (0.89)
  Pallas kernels: 51.8 us -> 47.4 us
  local copies, waits for them, and re-layouts: 2.67 us -> 1.22 us
    pallas_call x1, Pallas kernels: 51.8 us -> 47.4 us  [per_device(): pl.pallas_call(kernel, out_shape=(jax.ShapeDtypeStruct((K, M * LANES), F3...]
    unnamed x2, local copies, waits for them, and re-layouts: 2.67 us -> 1.22 us
where the time goes in v3:
time: 49.3 us; the launch traced here: 49.2 us
  Pallas kernels  47.4 us (96%)
  local copies, waits for them, and re-layouts  1.22 us (2%)
  between operations  0.64 us (1%)
    pallas_call x1, Pallas kernels, per_device(): pl.pallas_call(kernel, out_shape=(jax.ShapeDtypeStruct((K, M * LANES), F3...  47.4 us
    unnamed x2, local copies, waits for them, and re-layouts  1.22 us

profile of v3, /device:TPU:1, one launch (start us, length us, event | category | flops | bytes accessed | tf_op | source)
XLA Modules:
  0.0 49.2 jit_solution(18162458617711125188)
XLA Ops:
  0.6 47.4 %lanczos.1 = (f32[8,1024]{1,0:T(8,128)S(1)}, f32[16,16]{1,0:T(8,128)S(1)}) custom-call(f32[8,1024]{1,0:T(8,128)} %x_hbm.1, bf16[1,1,128,128,128]{4,3,2,1,0:T(8,128)(2,1)} %blocks.1, s32[16,1,128]{2,1,0:T(1,128)} %rows_hbm.1, s32[16,1,128]{2,1,0:T(1,128)} %cols_hbm.1, s32[8,16]{1,0:T(8,128)} %bitcast.1), custom_call_target="tpu_custom_call" | custom-call | tf_op jit(solution)/shard_map/lanczos/pallas_call | solution.py:408
  48.0 0.6 %copy.9 = f32[8,1024]{1,0:T(8,128)} copy(f32[8,1024]{1,0:T(8,128)S(1)} %get-tuple-element.4) | data formatting | bytes 65536
  48.6 0.6 %copy.10 = f32[16,16]{1,0:T(8,128)} copy(f32[16,16]{1,0:T(8,128)S(1)} %get-tuple-element.5) | data formatting | bytes 2048

commit v4 on v3

--- a/solution.py
+++ b/solution.py
@@ -1,4 +1,3 @@
-import functools
 import math
 
 import jax
@@ -21,8 +20,9 @@
 SLOTS = 128
 BATCH = 4
 UNROLL = 16
-SUM_C = BF16
-SUM_R = BF16
+I16 = jnp.int16
+TOP = 32700.0
+TINY = 1e-30
 
 
 def bcast(x):
@@ -32,8 +32,9 @@
 def kernel(
     x_hbm, blocks, rows_hbm, cols_hbm, counts_hbm,
     next_out, tri_out,
-    bl, blt, x_in, rows_s, cols_s, counts_s, rows_v, cols_v, xb, yb, xr, xc, yr, yc, picks_r, picks_c, res_d, res_t,
-    tot_r, tot_c, in_r, in_c, ykb, qown, wbuf, msg, ar, first, first_r, first_c,
+    bl, blt, x_in, rows_s, cols_s, counts_s, rows_v, cols_v, xb, yb, yraw, zb, wb, q1, q2,
+    own_q, own_s, seg_qr, seg_sr, seg_qc, seg_sc, spread, vr, vc, picks_r, picks_c, most, res_d, res_t,
+    tot_r, tot_c, sum_sr, sum_sc, in_r, in_c, in_sr, in_sc, ykb, msg, ar, first, first_r, first_c,
     load_sem, send_sem, recv_sem,
 ):
     r = lax.axis_index("row")
@@ -122,12 +123,14 @@
         for rr in row_peers:
             send(first.at[0], first_r.at[r], 18, (rr, c))
 
-    def first_reduce_finish():
+    def first_reduce_turn():
         wait_bytes(first_r.at[pl.ds(0, NR - 1)], recv_sem.at[18])
         first_r[r] = first[0]
         first[1] = tree([first_r[i] for i in range(NR)])
         for cc in col_peers:
             send(first.at[1], first_c.at[c], 19, (r, cc))
+
+    def first_reduce_finish():
         wait_bytes(first_c.at[pl.ds(0, NC - 1)], recv_sem.at[19])
         first_c[c] = first[1]
         return bcast(tree([first_c[i] for i in range(NC)]))
@@ -135,10 +138,10 @@
     def reduce_start(n, tile):
         msg[n] = jnp.sum(tile, axis=0, keepdims=True)
         for dev in others:
-            send(msg.at[n], ar.at[n, r * NC + c], 6 * n, dev)
+            send(msg.at[n], ar.at[n, r * NC + c], 16 + n, dev)
 
     def reduce_finish(n):
-        wait_bytes(ar.at[n, pl.ds(0, NR * NC - 1)], recv_sem.at[6 * n])
+        wait_bytes(ar.at[n, pl.ds(0, NR * NC - 1)], recv_sem.at[16 + n])
         ar[n, r * NC + c] = msg[n]
         sums = [ar[n, i] for i in range(8)]
         for i in range(8, NR * NC):
@@ -191,103 +194,158 @@
             acc = acc + cols[j] * ref[i, pl.ds(j, 1), :]
         return acc
 
-    def gather_start(src, seg_r, seg_c, n):
-        for cc in col_peers:
-            send(src, seg_r.at[pl.ds(M * c, M)], 6 * n + 3, (r, cc))
-        for rr in row_peers:
-            send(src, seg_c.at[pl.ds(M * r, M)], 6 * n + 2, (rr, c))
-        for b in range(M):
-            seg_c[M * r + b] = src[b]
-            seg_r[M * c + b] = src[b]
-
-    def gather_wait_col(seg_r, n):
-        wait_bytes(seg_r.at[pl.ds(0, (NC - 1) * M)], recv_sem.at[6 * n + 3])
-
-    def gather_wait_row(seg_c, n):
-        wait_bytes(seg_c.at[pl.ds(0, (NR - 1) * M)], recv_sem.at[6 * n + 2])
-
     zero = jnp.zeros((K, LANES), F32)
+    zero_pair = jnp.zeros((2 * K, LANES), BF16)
 
     def cat(a, b, axis):
         return jnp.concatenate([a, b], axis=axis)
 
+    def fixed(value):
+        return jnp.round(value).astype(jnp.int32).astype(I16)
+
+    def scales(largest):
+        m = jnp.maximum(bcast(jnp.max(largest, axis=1, keepdims=True)), TINY)
+        return TOP / m, m * (1.0 / TOP)
+
+    def to_row(scale):
+        return jnp.sum(jnp.where(lane_iota == row_iota, scale, 0.0), axis=0, keepdims=True)
+
+    def unpack_scales(row_ref, col_ref):
+        for i in range(NC):
+            spread[i] = picked(bcast(row_ref[i]), row_iota)
+        for i in range(NR):
+            spread[NC + i] = picked(bcast(col_ref[i]), row_iota)
+
+    def quantise(src, n):
+        largest = jnp.abs(src[0])
+        for b in range(1, M):
+            largest = jnp.maximum(largest, jnp.abs(src[b]))
+        inv, scale = scales(largest)
+        for bb in range(M // 2):
+            own_q[n, bb] = fixed(cat(src[2 * bb] * inv, src[2 * bb + 1] * inv, 0))
+        own_s[n] = to_row(scale)
+
+    def gather_start(n):
+        for cc in col_peers:
+            send(own_s.at[n], seg_sr.at[n, c], 8 * n + 0, (r, cc))
+            send(own_q.at[n], seg_qr.at[n, c], 8 * n + 1, (r, cc))
+        for rr in row_peers:
+            send(own_s.at[n], seg_sc.at[n, r], 8 * n + 2, (rr, c))
+            send(own_q.at[n], seg_qc.at[n, r], 8 * n + 3, (rr, c))
+        seg_sr[n, c] = own_s[n]
+        seg_qr[n, c] = own_q[n]
+        seg_sc[n, r] = own_s[n]
+        seg_qc[n, r] = own_q[n]
+
+    def split(pieces, quant, scale_row, vec, group):
+        def body(i, carry):
+            for u in range(group):
+                p = group * i + u
+                scale = picked(bcast(scale_row[p]), row_iota)
+                for bb in range(M // 2):
+                    both = quant[p, bb].astype(jnp.int32).astype(F32)
+                    for h in range(2):
+                        value = both[K * h : K * h + K] * scale
+                        high = value.astype(BF16).astype(F32)
+                        vec[M * p + 2 * bb + h] = cat(value, value - high, 0).astype(BF16)
+            return carry
+
+        lax.fori_loop(0, pieces // group, body, 0)
+
+    def gather_row_segment(n):
+        wait_bytes(seg_sr.at[n, pl.ds(0, NC - 1)], recv_sem.at[8 * n + 0])
+        wait_bytes(seg_qr.at[n, pl.ds(0, NC - 1)], recv_sem.at[8 * n + 1])
+        split(NC, seg_qr.at[n], seg_sr.at[n], vr, 4)
+
+    def gather_col_segment(n):
+        wait_bytes(seg_sc.at[n, pl.ds(0, NR - 1)], recv_sem.at[8 * n + 2])
+        wait_bytes(seg_qc.at[n, pl.ds(0, NR - 1)], recv_sem.at[8 * n + 3])
+        split(NR, seg_qc.at[n], seg_sc.at[n], vc, 4)
+
     def product(vec, ids, mats, res):
-        def body(q, carry):
+        count = counts_s[c, r]
+
+        def body(q, largest):
             base = BATCH * q
             b = [mats[base + i] for i in range(BATCH)]
             tile = cat(cat(b[0], b[1], 0), cat(b[2], b[3], 0), 1)
             x = [vec[ids[0, base + i]] for i in range(BATCH)]
             lhs = jnp.concatenate(
-                [cat(zero, x[i], 1) if i % 2 else cat(x[i], zero, 1) for i in range(BATCH)], axis=0
-            ).astype(BF16)
+                [
+                    cat(zero_pair, x[i], 1) if i % 2 else cat(x[i], zero_pair, 1)
+                    for i in range(BATCH)
+                ],
+                axis=0,
+            )
             out = jnp.dot(lhs, tile, preferred_element_type=F32)
             for i in range(BATCH):
                 half = LANES * (i // 2)
-                res[pl.ds(base + i, K, stride=SLOTS), :] = out[K * i : K * i + K, half : half + LANES]
-            return carry
-
-        lax.fori_loop(0, SLOTS // BATCH, body, 0, unroll=UNROLL)
-
-    def scatter(pick, res, put):
+                part = out[2 * K * i : 2 * K * i + 2 * K, half : half + LANES]
+                part = part[:K] + part[K:]
+                res[pl.ds(base + i, K, stride=SLOTS), :] = part
+                largest = jnp.maximum(largest, jnp.where(base + i < count, jnp.abs(part), 0.0))
+            return largest
+
+        return lax.fori_loop(0, SLOTS // BATCH, body, zero, unroll=UNROLL)
+
+    def scatter(pick, res, largest, bound, tot, pieces):
+        inv, scale = scales(largest * bound)
         for kk in range(K // 2):
             full = cat(
                 res[pl.ds(2 * kk * SLOTS, SLOTS), :], res[pl.ds((2 * kk + 1) * SLOTS, SLOTS), :], 1
             )
             hi = full.astype(BF16)
             lo = (full - hi.astype(F32)).astype(BF16)
-            put(kk, jnp.dot(pick[...], cat(hi, lo, 0), preferred_element_type=F32))
-
-    def exchange_cols(n):
-        def put(kk, out):
-            for i in range(NR):
+            out = jnp.dot(pick[...], cat(hi, lo, 0), preferred_element_type=F32)
+            even = bcast(inv[2 * kk : 2 * kk + 1, :])
+            odd = bcast(inv[2 * kk + 1 : 2 * kk + 2, :])
+            for i in range(pieces):
                 rows = out[M * i : M * i + M]
-                tot_c[n, i, kk] = cat(rows[:, :LANES], rows[:, LANES:], 0).astype(tot_c.dtype)
-
-        scatter(picks_c, res_t, put)
+                tot[i, kk] = fixed(cat(rows[:, :LANES] * even, rows[:, LANES:] * odd, 0))
+        return to_row(scale)
+
+    def exchange_cols(n, largest):
+        sum_sc[n] = scatter(picks_c, res_t, largest, most[1], tot_c.at[n], NR)
         for rr in row_peers:
-            send(tot_c.at[n, rr], in_c.at[n, r], 6 * n + 4, (rr, c))
+            send(sum_sc.at[n], in_sc.at[n, r], 8 * n + 4, (rr, c))
+            send(tot_c.at[n, rr], in_c.at[n, r], 8 * n + 5, (rr, c))
+        in_sc[n, r] = sum_sc[n]
         in_c[n, r] = tot_c[n, r]
 
-    def exchange_rows(n):
-        def put(kk, out):
-            for i in range(NC):
-                rows = out[M * i : M * i + M]
-                tot_r[n, i, kk] = cat(rows[:, :LANES], rows[:, LANES:], 0).astype(tot_r.dtype)
-
-        scatter(picks_r, res_d, put)
+    def exchange_rows(n, largest):
+        sum_sr[n] = scatter(picks_r, res_d, largest, most[0], tot_r.at[n], NC)
         for cc in col_peers:
-            send(tot_r.at[n, cc], in_r.at[n, c], 6 * n + 5, (r, cc))
+            send(sum_sr.at[n], in_sr.at[n, c], 8 * n + 6, (r, cc))
+            send(tot_r.at[n, cc], in_r.at[n, c], 8 * n + 7, (r, cc))
+        in_sr[n, c] = sum_sr[n]
         in_r[n, c] = tot_r[n, c]
 
     def exchange_finish(n, out_ref):
-        wait_bytes(in_r.at[n, pl.ds(0, NC - 1)], recv_sem.at[6 * n + 5])
+        wait_bytes(in_sr.at[n, pl.ds(0, NC - 1)], recv_sem.at[8 * n + 6])
+        wait_bytes(in_sc.at[n, pl.ds(0, NR - 1)], recv_sem.at[8 * n + 4])
+        unpack_scales(in_sr.at[n], in_sc.at[n])
+
+        def term(ref, i, kk, at):
+            even = bcast(spread[at + i, pl.ds(2 * kk, 1), :])
+            odd = bcast(spread[at + i, pl.ds(2 * kk + 1, 1), :])
+            return ref[n, i, kk].astype(jnp.int32).astype(F32) * cat(even, odd, 0)
+
+        wait_bytes(in_r.at[n, pl.ds(0, NC - 1)], recv_sem.at[8 * n + 7])
+        wait_bytes(in_c.at[n, pl.ds(0, NR - 1)], recv_sem.at[8 * n + 5])
         for kk in range(K // 2):
-            total = in_r[n, 0, kk].astype(F32)
-            for i in range(1, NC):
-                total = total + in_r[n, i, kk].astype(F32)
-            ykb[pl.ds(2 * M * kk, 2 * M), :] = total
-        wait_bytes(in_c.at[n, pl.ds(0, NR - 1)], recv_sem.at[6 * n + 4])
-        for kk in range(K // 2):
-            total = ykb[pl.ds(2 * M * kk, 2 * M), :]
-            for i in range(NR):
-                total = total + in_c[n, i, kk].astype(F32)
-            ykb[pl.ds(2 * M * kk, 2 * M), :] = total
+            terms = [term(in_r, i, kk, 0) for i in range(NC)]
+            total = tree(terms)
+            terms = [term(in_c, i, kk, NC) for i in range(NR)]
+            ykb[pl.ds(2 * M * kk, 2 * M), :] = total + tree(terms)
         for b in range(M):
             out_ref[b] = ykb[pl.ds(b, K, stride=M), :]
-
-    def sweep(count, step, update):
-        def body(i, carry):
-            for u in range(step):
-                update(step * i + u)
-            return carry
-
-        lax.fori_loop(0, count // step, body, 0)
 
     for load in small:
         load.wait()
     for b in range(M):
         xb[b] = x_in[:, pl.ds(LANES * b, LANES)]
     start_tile = gram(xb, xb, 0, zero)
+    quantise(xb, 0)
 
     giota = lax.broadcasted_iota(jnp.int32, (1, SLOTS), 1)
     row_ids = rows_v[...]
@@ -300,6 +358,8 @@
     want_c = jnp.where(mirror, col_ids, -1)
     one_r = jnp.where(lax.broadcasted_iota(jnp.int32, (RB, SLOTS), 0) == want_r, 1.0, 0.0)
     one_c = jnp.where(lax.broadcasted_iota(jnp.int32, (CB, SLOTS), 0) == want_c, 1.0, 0.0)
+    for i, one in enumerate((one_r, one_c)):
+        most[i] = bcast(jnp.max(jnp.sum(one, axis=1, keepdims=True), axis=0, keepdims=True))
     one_r = one_r.astype(BF16)
     one_c = one_c.astype(BF16)
     picks_r[...] = cat(one_r, one_r, 1)
@@ -308,7 +368,7 @@
     pl.semaphore_wait(barrier, NR + NC - 2)
 
     first_reduce_start(start_tile)
-    gather_start(xb, xr, xc, 0)
+    gather_start(0)
     for load in loads:
         load.wait()
 
@@ -318,70 +378,67 @@
         return carry
 
     lax.fori_loop(0, SLOTS // 8, turn, 0)
+
+    gather_row_segment(0)
+    largest = product(vr, rows_s, bl, res_t)
+    exchange_cols(0, largest)
+    first_reduce_turn()
+    gather_col_segment(0)
+    largest = product(vc, cols_s, blt, res_d)
+    exchange_rows(0, largest)
     inverse, _, _ = factor(columns(first_reduce_finish(), 0))
-
-    def normalise(seg, t):
-        seg[t] = apply(inverse, seg, t)
-
-    gather_wait_col(xr, 0)
-    sweep(RB, 8, functools.partial(normalise, xr))
-    product(xr, rows_s, bl, res_t)
-    exchange_cols(0)
-    gather_wait_row(xc, 0)
-    sweep(CB, 8, functools.partial(normalise, xc))
-    product(xc, cols_s, blt, res_d)
-    exchange_rows(0)
     for b in range(M):
-        qown[0, b] = xr[M * c + b]
-    exchange_finish(0, yb)
-
-    tile = gram(yb, qown.at[0], 0, zero)
+        q1[b] = apply(inverse, xb, b)
+    exchange_finish(0, yraw)
+    for b in range(M):
+        yb[b] = apply(inverse, yraw, b)
+
+    quantise(yb, 1)
+    gather_start(1)
+    tile = gram(yb, q1, 0, zero)
     tile = gram(yb, yb, K, tile)
-    reduce_start(1, tile)
-    gather_start(yb, yr, yc, 1)
-    total = reduce_finish(1)
+    reduce_start(0, tile)
+    gather_row_segment(1)
+    largest = product(vr, rows_s, bl, res_t)
+    exchange_cols(1, largest)
+    gather_col_segment(1)
+    largest = product(vc, cols_s, blt, res_d)
+    exchange_rows(1, largest)
+    total = reduce_finish(0)
     at_cols = columns(total, 0)
     s_cols = columns(total, K)
     a1_cols = rows_of(total)
     ata = matmul_cols(at_cols, a1_cols)
     inverse, upper1, lower1 = factor([s - t for s, t in zip(s_cols, ata)])
     back = matmul_cols(inverse, at_cols)
-
-    def advance(seg, old, t):
-        seg[t] = apply(inverse, seg, t) - apply(back, old, t)
-
-    gather_wait_col(yr, 1)
-    sweep(RB, 4, functools.partial(advance, yr, xr))
-    product(yr, rows_s, bl, res_t)
-    exchange_cols(1)
-    gather_wait_row(yc, 1)
-    sweep(CB, 4, functools.partial(advance, yc, xc))
-    product(yc, cols_s, blt, res_d)
-    exchange_rows(1)
     for b in range(M):
-        qown[1, b] = yr[M * c + b]
+        q2[b] = apply(inverse, yb, b) - apply(back, q1, b)
+        wb[b] = apply(back, yb, b) + apply(upper1, q1, b)
     top = zero
     for j in range(K):
         top = jnp.where(lane_iota == j, a1_cols[j], top)
         top = jnp.where(lane_iota == K + j, lower1[j], top)
     tri_out[pl.ds(0, K), :] = top[:, : 2 * K]
-    exchange_finish(1, wbuf)
+    exchange_finish(1, zb)
     for b in range(M):
-        wbuf[b] = wbuf[b] - apply(upper1, qown.at[0], b)
-    tile = gram(wbuf, qown.at[1], 0, zero)
-    tile = gram(wbuf, wbuf, K, tile)
-    reduce_start(2, tile)
+        wb[b] = apply(inverse, zb, b) - wb[b]
+    tile = gram(wb, q2, 0, zero)
+    tile = gram(wb, wb, K, tile)
+    reduce_start(1, tile)
 
     wait_bytes(first_r.at[pl.ds(0, NR - 1)], send_sem.at[18])
     wait_bytes(first_c.at[pl.ds(0, NC - 1)], send_sem.at[19])
-    wait_bytes(ar.at[1, pl.ds(0, NR * NC - 1)], send_sem.at[6])
+    wait_bytes(ar.at[0, pl.ds(0, NR * NC - 1)], send_sem.at[16])
     for n in range(2):
-        wait_bytes(xc.at[pl.ds(0, (NR - 1) * M)], send_sem.at[6 * n + 2])
-        wait_bytes(xr.at[pl.ds(0, (NC - 1) * M)], send_sem.at[6 * n + 3])
-        wait_bytes(in_c.at[n, pl.ds(0, NR - 1)], send_sem.at[6 * n + 4])
-        wait_bytes(in_r.at[n, pl.ds(0, NC - 1)], send_sem.at[6 * n + 5])
-
-    total = reduce_finish(2)
+        for i, (ref, count) in enumerate(
+            [
+                (seg_sr, NC), (seg_qr, NC), (seg_sc, NR), (seg_qc, NR),
+                (in_sc, NR), (in_c, NR), (in_sr, NC), (in_r, NC),
+            ]
+        ):
+            wait_bytes(ref.at[n, pl.ds(0, count - 1)], send_sem.at[8 * n + i])
+
+    total = reduce_finish(1)
     at_cols = columns(total, 0)
     s_cols = columns(total, K)
     a2_cols = rows_of(total)
@@ -390,14 +447,14 @@
     back = matmul_cols(inverse, at_cols)
     order_root = math.sqrt(NR * NC * M * LANES)
     for b in range(M):
-        value = apply(inverse, wbuf, b) - apply(back, qown.at[1], b)
+        value = apply(inverse, wb, b) - apply(back, q2, b)
         next_out[:, pl.ds(LANES * b, LANES)] = value * order_root
     low = zero
     for j in range(K):
         low = jnp.where(lane_iota == j, upper1[j], low)
         low = jnp.where(lane_iota == K + j, a2_cols[j], low)
     tri_out[pl.ds(K, K), :] = low[:, : 2 * K]
-    wait_bytes(ar.at[2, pl.ds(0, NR * NC - 1)], send_sem.at[12])
+    wait_bytes(ar.at[1, pl.ds(0, NR * NC - 1)], send_sem.at[17])
 
 
 def per_device(start_block, blocks, block_rows, block_cols, counts):
@@ -405,6 +462,7 @@
     vmem = pl.BlockSpec(memory_space=pltpu.VMEM)
     hbm = pl.BlockSpec(memory_space=pltpu.HBM)
     tile = (K, LANES)
+    pair = (2 * K, LANES)
     return pl.pallas_call(
         kernel,
         out_shape=(
@@ -422,25 +480,32 @@
             pltpu.SMEM((NC, NR), jnp.int32),
             pltpu.VMEM((1, SLOTS), jnp.int32),
             pltpu.VMEM((1, SLOTS), jnp.int32),
-            pltpu.VMEM((M, *tile), F32),
-            pltpu.VMEM((M, *tile), F32),
-            pltpu.VMEM((RB, *tile), F32),
-            pltpu.VMEM((CB, *tile), F32),
-            pltpu.VMEM((RB, *tile), F32),
-            pltpu.VMEM((CB, *tile), F32),
+            *[pltpu.VMEM((M, *tile), F32)] * 7,
+            pltpu.VMEM((2, M // 2, *pair), I16),
+            pltpu.VMEM((2, 1, LANES), F32),
+            pltpu.VMEM((2, NC, M // 2, *pair), I16),
+            pltpu.VMEM((2, NC, 1, LANES), F32),
+            pltpu.VMEM((2, NR, M // 2, *pair), I16),
+            pltpu.VMEM((2, NR, 1, LANES), F32),
+            pltpu.VMEM((NC + NR, *tile), F32),
+            pltpu.VMEM((RB, *pair), BF16),
+            pltpu.VMEM((CB, *pair), BF16),
             pltpu.VMEM((RB, 2 * SLOTS), BF16),
             pltpu.VMEM((CB, 2 * SLOTS), BF16),
+            pltpu.VMEM((2, *tile), F32),
             pltpu.VMEM((K * SLOTS, LANES), F32),
             pltpu.VMEM((K * SLOTS, LANES), F32),
-            pltpu.VMEM((2, NC, K // 2, 2 * M, LANES), SUM_R),
-            pltpu.VMEM((2, NR, K // 2, 2 * M, LANES), SUM_C),
-            pltpu.VMEM((2, NC, K // 2, 2 * M, LANES), SUM_R),
-            pltpu.VMEM((2, NR, K // 2, 2 * M, LANES), SUM_C),
+            pltpu.VMEM((2, NC, K // 2, *pair), I16),
+            pltpu.VMEM((2, NR, K // 2, *pair), I16),
+            pltpu.VMEM((2, 1, LANES), F32),
+            pltpu.VMEM((2, 1, LANES), F32),
+            pltpu.VMEM((2, NC, K // 2, *pair), I16),
+            pltpu.VMEM((2, NR, K // 2, *pair), I16),
+            pltpu.VMEM((2, NC, 1, LANES), F32),
+            pltpu.VMEM((2, NR, 1, LANES), F32),
             pltpu.VMEM((K * M, LANES), F32),
-            pltpu.VMEM((2, M, *tile), F32),
-            pltpu.VMEM((M, *tile), F32),
-            pltpu.VMEM((3, 1, LANES), F32),
-            pltpu.VMEM((3, NR * NC, 1, LANES), F32),
+            pltpu.VMEM((2, 1, LANES), F32),
+            pltpu.VMEM((2, NR * NC, 1, LANES), F32),
             pltpu.VMEM((2, 1, LANES), F32),
             pltpu.VMEM((NR, 1, LANES), F32),
             pltpu.VMEM((NC, 1, LANES), F32),

time: 49.3 us -> 40.7 us (0.83)
  Pallas kernels: 47.4 us -> 38.7 us
    pallas_call x1, Pallas kernels: 47.4 us -> 38.7 us  [per_device(): pl.pallas_call(kernel, out_shape=(jax.ShapeDtypeStruct((K, M * LANES), F3...]
where the time goes in v4:
time: 40.7 us; the launch traced here: 40.6 us
  Pallas kernels  38.7 us (95%)
  local copies, waits for them, and re-layouts  1.22 us (3%)
  between operations  0.64 us (2%)
    pallas_call x1, Pallas kernels, per_device(): pl.pallas_call(kernel, out_shape=(jax.ShapeDtypeStruct((K, M * LANES), F3...  38.7 us
    unnamed x2, local copies, waits for them, and re-layouts  1.22 us

profile of v4, /device:TPU:1, one launch (start us, length us, event | category | flops | bytes accessed | tf_op | source)
XLA Modules:
  0.0 40.6 jit_solution(13358499254873664801)
XLA Ops:
  0.6 38.7 %lanczos.1 = (f32[8,1024]{1,0:T(8,128)S(1)}, f32[16,16]{1,0:T(8,128)S(1)}) custom-call(f32[8,1024]{1,0:T(8,128)} %x_hbm.1, bf16[1,1,128,128,128]{4,3,2,1,0:T(8,128)(2,1)} %blocks.1, s32[16,1,128]{2,1,0:T(1,128)} %rows_hbm.1, s32[16,1,128]{2,1,0:T(1,128)} %cols_hbm.1, s32[8,16]{1,0:T(8,128)} %bitcast.1), custom_call_target="tpu_custom_call" | custom-call | tf_op jit(solution)/shard_map/lanczos/pallas_call | solution.py:466
  39.4 0.6 %copy.9 = f32[8,1024]{1,0:T(8,128)} copy(f32[8,1024]{1,0:T(8,128)S(1)} %get-tuple-element.4) | data formatting | bytes 65536
  40.0 0.6 %copy.10 = f32[16,16]{1,0:T(8,128)} copy(f32[16,16]{1,0:T(8,128)S(1)} %get-tuple-element.5) | data formatting | bytes 2048

commit v5 on v4

--- a/solution.py
+++ b/solution.py
@@ -19,7 +19,7 @@
 RB, CB = NC * M, NR * M
 SLOTS = 128
 BATCH = 4
-UNROLL = 16
+UNROLL = 32
 I16 = jnp.int16
 TOP = 32700.0
 TINY = 1e-30
@@ -210,11 +210,9 @@
     def to_row(scale):
         return jnp.sum(jnp.where(lane_iota == row_iota, scale, 0.0), axis=0, keepdims=True)
 
-    def unpack_scales(row_ref, col_ref):
-        for i in range(NC):
-            spread[i] = picked(bcast(row_ref[i]), row_iota)
-        for i in range(NR):
-            spread[NC + i] = picked(bcast(col_ref[i]), row_iota)
+    def unpack_scales(ref, count, at):
+        for i in range(count):
+            spread[at + i] = picked(bcast(ref[i]), row_iota)
 
     def quantise(src, n):
         largest = jnp.abs(src[0])
@@ -228,20 +226,22 @@
     def gather_start(n):
         for cc in col_peers:
             send(own_s.at[n], seg_sr.at[n, c], 8 * n + 0, (r, cc))
+        for cc in col_peers:
             send(own_q.at[n], seg_qr.at[n, c], 8 * n + 1, (r, cc))
         for rr in row_peers:
             send(own_s.at[n], seg_sc.at[n, r], 8 * n + 2, (rr, c))
+        for rr in row_peers:
             send(own_q.at[n], seg_qc.at[n, r], 8 * n + 3, (rr, c))
         seg_sr[n, c] = own_s[n]
         seg_qr[n, c] = own_q[n]
         seg_sc[n, r] = own_s[n]
         seg_qc[n, r] = own_q[n]
 
-    def split(pieces, quant, scale_row, vec, group):
+    def split(pieces, quant, at, vec, group):
         def body(i, carry):
             for u in range(group):
                 p = group * i + u
-                scale = picked(bcast(scale_row[p]), row_iota)
+                scale = spread[at + p]
                 for bb in range(M // 2):
                     both = quant[p, bb].astype(jnp.int32).astype(F32)
                     for h in range(2):
@@ -254,13 +254,15 @@
 
     def gather_row_segment(n):
         wait_bytes(seg_sr.at[n, pl.ds(0, NC - 1)], recv_sem.at[8 * n + 0])
+        unpack_scales(seg_sr.at[n], NC, 0)
         wait_bytes(seg_qr.at[n, pl.ds(0, NC - 1)], recv_sem.at[8 * n + 1])
-        split(NC, seg_qr.at[n], seg_sr.at[n], vr, 4)
+        split(NC, seg_qr.at[n], 0, vr, 4)
 
     def gather_col_segment(n):
         wait_bytes(seg_sc.at[n, pl.ds(0, NR - 1)], recv_sem.at[8 * n + 2])
+        unpack_scales(seg_sc.at[n], NR, NC)
         wait_bytes(seg_qc.at[n, pl.ds(0, NR - 1)], recv_sem.at[8 * n + 3])
-        split(NR, seg_qc.at[n], seg_sc.at[n], vc, 4)
+        split(NR, seg_qc.at[n], NC, vc, 4)
 
     def product(vec, ids, mats, res):
         count = counts_s[c, r]
@@ -288,8 +290,7 @@
 
         return lax.fori_loop(0, SLOTS // BATCH, body, zero, unroll=UNROLL)
 
-    def scatter(pick, res, largest, bound, tot, pieces):
-        inv, scale = scales(largest * bound)
+    def scatter(pick, res, inv, tot, pieces):
         for kk in range(K // 2):
             full = cat(
                 res[pl.ds(2 * kk * SLOTS, SLOTS), :], res[pl.ds((2 * kk + 1) * SLOTS, SLOTS), :], 1
@@ -302,20 +303,25 @@
             for i in range(pieces):
                 rows = out[M * i : M * i + M]
                 tot[i, kk] = fixed(cat(rows[:, :LANES] * even, rows[:, LANES:] * odd, 0))
-        return to_row(scale)
 
     def exchange_cols(n, largest):
-        sum_sc[n] = scatter(picks_c, res_t, largest, most[1], tot_c.at[n], NR)
+        inv, scale = scales(largest * most[1])
+        sum_sc[n] = to_row(scale)
         for rr in row_peers:
             send(sum_sc.at[n], in_sc.at[n, r], 8 * n + 4, (rr, c))
+        scatter(picks_c, res_t, inv, tot_c.at[n], NR)
+        for rr in row_peers:
             send(tot_c.at[n, rr], in_c.at[n, r], 8 * n + 5, (rr, c))
         in_sc[n, r] = sum_sc[n]
         in_c[n, r] = tot_c[n, r]
 
     def exchange_rows(n, largest):
-        sum_sr[n] = scatter(picks_r, res_d, largest, most[0], tot_r.at[n], NC)
+        inv, scale = scales(largest * most[0])
+        sum_sr[n] = to_row(scale)
         for cc in col_peers:
             send(sum_sr.at[n], in_sr.at[n, c], 8 * n + 6, (r, cc))
+        scatter(picks_r, res_d, inv, tot_r.at[n], NC)
+        for cc in col_peers:
             send(tot_r.at[n, cc], in_r.at[n, c], 8 * n + 7, (r, cc))
         in_sr[n, c] = sum_sr[n]
         in_r[n, c] = tot_r[n, c]
@@ -323,7 +329,8 @@
     def exchange_finish(n, out_ref):
         wait_bytes(in_sr.at[n, pl.ds(0, NC - 1)], recv_sem.at[8 * n + 6])
         wait_bytes(in_sc.at[n, pl.ds(0, NR - 1)], recv_sem.at[8 * n + 4])
-        unpack_scales(in_sr.at[n], in_sc.at[n])
+        unpack_scales(in_sr.at[n], NC, 0)
+        unpack_scales(in_sc.at[n], NR, NC)
 
         def term(ref, i, kk, at):
             even = bcast(spread[at + i, pl.ds(2 * kk, 1), :])
@@ -331,12 +338,13 @@
             return ref[n, i, kk].astype(jnp.int32).astype(F32) * cat(even, odd, 0)
 
         wait_bytes(in_r.at[n, pl.ds(0, NC - 1)], recv_sem.at[8 * n + 7])
+        for kk in range(K // 2):
+            terms = [term(in_r, i, kk, 0) for i in range(NC)]
+            ykb[pl.ds(2 * M * kk, 2 * M), :] = tree(terms)
         wait_bytes(in_c.at[n, pl.ds(0, NR - 1)], recv_sem.at[8 * n + 5])
         for kk in range(K // 2):
-            terms = [term(in_r, i, kk, 0) for i in range(NC)]
-            total = tree(terms)
             terms = [term(in_c, i, kk, NC) for i in range(NR)]
-            ykb[pl.ds(2 * M * kk, 2 * M), :] = total + tree(terms)
+            ykb[pl.ds(2 * M * kk, 2 * M), :] += tree(terms)
         for b in range(M):
             out_ref[b] = ykb[pl.ds(b, K, stride=M), :]
 
@@ -457,13 +465,24 @@
     wait_bytes(ar.at[1, pl.ds(0, NR * NC - 1)], send_sem.at[17])
 
 
+def write_out(block, projection, block_out, projection_out, sems):
+    copies = [
+        pltpu.make_async_copy(block, block_out, sems.at[0]),
+        pltpu.make_async_copy(projection, projection_out, sems.at[1]),
+    ]
+    for copy in copies:
+        copy.start()
+    for copy in copies:
+        copy.wait()
+
+
 def per_device(start_block, blocks, block_rows, block_cols, counts):
     args = (start_block, blocks, block_rows, block_cols, counts.T)
     vmem = pl.BlockSpec(memory_space=pltpu.VMEM)
     hbm = pl.BlockSpec(memory_space=pltpu.HBM)
     tile = (K, LANES)
     pair = (2 * K, LANES)
-    return pl.pallas_call(
+    block, projection = pl.pallas_call(
         kernel,
         out_shape=(
             jax.ShapeDtypeStruct((K, M * LANES), F32),
@@ -518,6 +537,20 @@
         ),
         name="lanczos",
     )(*[pltpu.with_memory_space_constraint(v, pltpu.HBM) for v in args])
+    return pl.pallas_call(
+        write_out,
+        out_shape=(
+            jax.ShapeDtypeStruct(block.shape, F32),
+            jax.ShapeDtypeStruct(projection.shape, F32),
+        ),
+        in_specs=[vmem, vmem],
+        out_specs=(hbm, hbm),
+        scratch_shapes=[pltpu.SemaphoreType.DMA((2,))],
+        name="write_out",
+    )(
+        pltpu.with_memory_space_constraint(block, pltpu.VMEM),
+        pltpu.with_memory_space_constraint(projection, pltpu.VMEM),
+    )
 
 
 def solution(mesh):

time: 40.7 us -> 39.5 us (0.971)
  local copies, waits for them, and re-layouts: 1.22 us -> 0 us
    unnamed x2 -> x0, local copies, waits for them, and re-layouts: 1.22 us -> none
    pallas_call x0 -> x1, Pallas kernels: none -> 0.64 us  [per_device(): pl.pallas_call(write_out, out_shape=(jax.ShapeDtypeStruct(block.shape, F3...]
    pallas_call x1, Pallas kernels: 38.7 us -> 38.1 us  [per_device(): pl.pallas_call(kernel, out_shape=(jax.ShapeDtypeStruct((K, M * LANES), F3...]
where the time goes in v5:
time: 39.5 us; the launch traced here: 39.4 us
  Pallas kernels  38.8 us (98%)
  between operations  0.64 us (2%)
    pallas_call x1, Pallas kernels, per_device(): pl.pallas_call(kernel, out_shape=(jax.ShapeDtypeStruct((K, M * LANES), F3...  38.1 us

profile of v5, /device:TPU:1, one launch (start us, length us, event | category | flops | bytes accessed | tf_op | source)
XLA Modules:
  0.0 39.4 jit_solution(3194055583024459210)
XLA Ops:
  0.6 38.1 %lanczos.1 = (f32[8,1024]{1,0:T(8,128)S(1)}, f32[16,16]{1,0:T(8,128)S(1)}) custom-call(f32[8,1024]{1,0:T(8,128)} %x_hbm.1, bf16[1,1,128,128,128]{4,3,2,1,0:T(8,128)(2,1)} %blocks.1, s32[16,1,128]{2,1,0:T(1,128)} %rows_hbm.1, s32[16,1,128]{2,1,0:T(1,128)} %cols_hbm.1, s32[8,16]{1,0:T(8,128)} %bitcast.1), custom_call_target="tpu_custom_call" | custom-call | tf_op jit(solution)/shard_map/lanczos/pallas_call | solution.py:485
  38.8 0.6 %write_out.1 = (f32[8,1024]{1,0:T(8,128)}, f32[16,16]{1,0:T(8,128)}) custom-call(f32[8,1024]{1,0:T(8,128)S(1)} %get-tuple-element.4.block, f32[16,16]{1,0:T(8,128)S(1)} %get-tuple-element.5.projection), custom_call_target="tpu_custom_call" | custom-call | tf_op jit(solution)/shard_map/write_out/pallas_call | solution.py:540

commit v6 on v5

--- a/solution.py
+++ b/solution.py
@@ -20,6 +20,7 @@
 SLOTS = 128
 BATCH = 4
 UNROLL = 32
+PITCH = 132
 I16 = jnp.int16
 TOP = 32700.0
 TINY = 1e-30
@@ -32,7 +33,7 @@
 def kernel(
     x_hbm, blocks, rows_hbm, cols_hbm, counts_hbm,
     next_out, tri_out,
-    bl, blt, x_in, rows_s, cols_s, counts_s, rows_v, cols_v, xb, yb, yraw, zb, wb, q1, q2,
+    bl, blt, x_in, ids_s, counts_s, ids_v, xb, yb, yraw, zb, wb, q1, q2,
     own_q, own_s, seg_qr, seg_sr, seg_qc, seg_sc, spread, vr, vc, picks_r, picks_c, most, res_d, res_t,
     tot_r, tot_c, sum_sr, sum_sc, in_r, in_c, in_sr, in_sc, ykb, msg, ar, first, first_r, first_c,
     load_sem, send_sem, recv_sem,
@@ -72,36 +73,47 @@
 
     parts = 4
     step = SLOTS // parts
+    small = [
+        pltpu.make_async_copy(src, dst, load_sem.at[i])
+        for src, dst, i in [
+            (x_hbm, x_in, 0),
+            (rows_hbm.at[r], ids_v.at[0], 1),
+            (cols_hbm.at[r], ids_v.at[1], 1),
+            (rows_hbm.at[r], ids_s.at[0], 2),
+            (cols_hbm.at[r], ids_s.at[1], 2),
+            (counts_hbm, counts_s, 3),
+        ]
+    ]
     loads = [
         pltpu.make_async_copy(
-            blocks.at[0, 0, pl.ds(i * step, step)], bl.at[pl.ds(i * step, step)], load_sem.at[i]
+            blocks.at[0, 0, pl.ds(i * step, step)], bl.at[pl.ds(i * step, step)], load_sem.at[4]
         )
         for i in range(parts)
     ]
-    small = [
-        pltpu.make_async_copy(src, dst, load_sem.at[parts + i])
-        for i, (src, dst) in enumerate(
-            [
-                (x_hbm, x_in),
-                (rows_hbm.at[r], rows_s),
-                (cols_hbm.at[r], cols_s),
-                (counts_hbm, counts_s),
-                (rows_hbm.at[r], rows_v),
-                (cols_hbm.at[r], cols_v),
-            ]
-        )
-    ]
     for load in small + loads:
         load.start()
 
     def send(src, dst, sems, dev):
+        kind = 2 if sems >= 18 else 1 if sems >= 16 else 1 - sems % 2
         pltpu.make_async_remote_copy(
-            src_ref=src, dst_ref=dst, send_sem=send_sem.at[sems], recv_sem=recv_sem.at[sems],
+            src_ref=src, dst_ref=dst, send_sem=send_sem.at[kind], recv_sem=recv_sem.at[sems],
             device_id=dev, device_id_type=MESH,
         ).start()
 
     def wait_bytes(ref, sem):
         pltpu.make_async_copy(ref, ref, sem).wait()
+
+    def send_if(wanted, *copy):
+        @pl.when(wanted)
+        def _():
+            send(*copy)
+
+    def wait_pieces(ref, sem, count):
+        for i in range(1, NR):
+
+            @pl.when(count == i)
+            def _():
+                wait_bytes(ref.at[pl.ds(0, i)], sem)
 
     def gram(a_ref, b_ref, lane0, tile):
         for j in range(K):
@@ -229,9 +241,9 @@
         for cc in col_peers:
             send(own_q.at[n], seg_qr.at[n, c], 8 * n + 1, (r, cc))
         for rr in row_peers:
-            send(own_s.at[n], seg_sc.at[n, r], 8 * n + 2, (rr, c))
+            send_if(rr > r, own_s.at[n], seg_sc.at[n, r], 8 * n + 2, (rr, c))
         for rr in row_peers:
-            send(own_q.at[n], seg_qc.at[n, r], 8 * n + 3, (rr, c))
+            send_if(rr > r, own_q.at[n], seg_qc.at[n, r], 8 * n + 3, (rr, c))
         seg_sr[n, c] = own_s[n]
         seg_qr[n, c] = own_q[n]
         seg_sc[n, r] = own_s[n]
@@ -258,20 +270,22 @@
         wait_bytes(seg_qr.at[n, pl.ds(0, NC - 1)], recv_sem.at[8 * n + 1])
         split(NC, seg_qr.at[n], 0, vr, 4)
 
+    def gather_col_scales(n):
+        wait_pieces(seg_sc.at[n], recv_sem.at[8 * n + 2], r)
+        unpack_scales(seg_sc.at[n], NR, NC)
+
     def gather_col_segment(n):
-        wait_bytes(seg_sc.at[n, pl.ds(0, NR - 1)], recv_sem.at[8 * n + 2])
-        unpack_scales(seg_sc.at[n], NR, NC)
-        wait_bytes(seg_qc.at[n, pl.ds(0, NR - 1)], recv_sem.at[8 * n + 3])
+        wait_pieces(seg_qc.at[n], recv_sem.at[8 * n + 3], r)
         split(NR, seg_qc.at[n], NC, vc, 4)
 
-    def product(vec, ids, mats, res):
+    def product(vec, which, mats, res):
         count = counts_s[c, r]
 
         def body(q, largest):
             base = BATCH * q
             b = [mats[base + i] for i in range(BATCH)]
             tile = cat(cat(b[0], b[1], 0), cat(b[2], b[3], 0), 1)
-            x = [vec[ids[0, base + i]] for i in range(BATCH)]
+            x = [vec[ids_s[which, 0, base + i]] for i in range(BATCH)]
             lhs = jnp.concatenate(
                 [
                     cat(zero_pair, x[i], 1) if i % 2 else cat(x[i], zero_pair, 1)
@@ -284,7 +298,7 @@
                 half = LANES * (i // 2)
                 part = out[2 * K * i : 2 * K * i + 2 * K, half : half + LANES]
                 part = part[:K] + part[K:]
-                res[pl.ds(base + i, K, stride=SLOTS), :] = part
+                res[pl.ds(base + i, K, stride=PITCH), :] = part
                 largest = jnp.maximum(largest, jnp.where(base + i < count, jnp.abs(part), 0.0))
             return largest
 
@@ -293,7 +307,7 @@
     def scatter(pick, res, inv, tot, pieces):
         for kk in range(K // 2):
             full = cat(
-                res[pl.ds(2 * kk * SLOTS, SLOTS), :], res[pl.ds((2 * kk + 1) * SLOTS, SLOTS), :], 1
+                res[pl.ds(2 * kk * PITCH, SLOTS), :], res[pl.ds((2 * kk + 1) * PITCH, SLOTS), :], 1
             )
             hi = full.astype(BF16)
             lo = (full - hi.astype(F32)).astype(BF16)
@@ -308,10 +322,10 @@
         inv, scale = scales(largest * most[1])
         sum_sc[n] = to_row(scale)
         for rr in row_peers:
-            send(sum_sc.at[n], in_sc.at[n, r], 8 * n + 4, (rr, c))
+            send_if(rr < r, sum_sc.at[n], in_sc.at[n, r], 8 * n + 4, (rr, c))
         scatter(picks_c, res_t, inv, tot_c.at[n], NR)
         for rr in row_peers:
-            send(tot_c.at[n, rr], in_c.at[n, r], 8 * n + 5, (rr, c))
+            send_if(rr < r, tot_c.at[n, rr], in_c.at[n, r], 8 * n + 5, (rr, c))
         in_sc[n, r] = sum_sc[n]
         in_c[n, r] = tot_c[n, r]
 
@@ -328,7 +342,7 @@
 
     def exchange_finish(n, out_ref):
         wait_bytes(in_sr.at[n, pl.ds(0, NC - 1)], recv_sem.at[8 * n + 6])
-        wait_bytes(in_sc.at[n, pl.ds(0, NR - 1)], recv_sem.at[8 * n + 4])
+        wait_pieces(in_sc.at[n], recv_sem.at[8 * n + 4], NR - 1 - r)
         unpack_scales(in_sr.at[n], NC, 0)
         unpack_scales(in_sc.at[n], NR, NC)
 
@@ -341,23 +355,23 @@
         for kk in range(K // 2):
             terms = [term(in_r, i, kk, 0) for i in range(NC)]
             ykb[pl.ds(2 * M * kk, 2 * M), :] = tree(terms)
-        wait_bytes(in_c.at[n, pl.ds(0, NR - 1)], recv_sem.at[8 * n + 5])
+        wait_pieces(in_c.at[n], recv_sem.at[8 * n + 5], NR - 1 - r)
         for kk in range(K // 2):
             terms = [term(in_c, i, kk, NC) for i in range(NR)]
             ykb[pl.ds(2 * M * kk, 2 * M), :] += tree(terms)
         for b in range(M):
             out_ref[b] = ykb[pl.ds(b, K, stride=M), :]
 
-    for load in small:
-        load.wait()
+    for i, ref in enumerate((x_in, ids_v, ids_s, counts_s)):
+        wait_bytes(ref, load_sem.at[i])
     for b in range(M):
         xb[b] = x_in[:, pl.ds(LANES * b, LANES)]
     start_tile = gram(xb, xb, 0, zero)
     quantise(xb, 0)
 
     giota = lax.broadcasted_iota(jnp.int32, (1, SLOTS), 1)
-    row_ids = rows_v[...]
-    col_ids = cols_v[...]
+    row_ids = ids_v[0]
+    col_ids = ids_v[1]
     valid = giota < counts_s[c, r]
     global_row = r * RB + row_ids
     global_col = ((col_ids // M) * NC + c) * M + lax.rem(col_ids, M)
@@ -377,8 +391,7 @@
 
     first_reduce_start(start_tile)
     gather_start(0)
-    for load in loads:
-        load.wait()
+    wait_bytes(bl, load_sem.at[4])
 
     def turn(i, carry):
         for u in range(8):
@@ -387,12 +400,24 @@
 
     lax.fori_loop(0, SLOTS // 8, turn, 0)
 
+    def clear(refs, i, wanted):
+        @pl.when(wanted)
+        def _():
+            for ref in refs:
+                for n in range(2):
+                    ref[n, i] = jnp.zeros_like(ref[n, i])
+
+    for i in range(NR):
+        clear((in_c, in_sc), i, r > i)
+        clear((seg_qc, seg_sc), i, r < i)
+
     gather_row_segment(0)
-    largest = product(vr, rows_s, bl, res_t)
+    largest = product(vr, 0, bl, res_t)
+    first_reduce_turn()
     exchange_cols(0, largest)
-    first_reduce_turn()
+    gather_col_scales(0)
     gather_col_segment(0)
-    largest = product(vc, cols_s, blt, res_d)
+    largest = product(vc, 1, blt, res_d)
     exchange_rows(0, largest)
     inverse, _, _ = factor(columns(first_reduce_finish(), 0))
     for b in range(M):
@@ -407,10 +432,11 @@
     tile = gram(yb, yb, K, tile)
     reduce_start(0, tile)
     gather_row_segment(1)
-    largest = product(vr, rows_s, bl, res_t)
+    largest = product(vr, 0, bl, res_t)
     exchange_cols(1, largest)
+    gather_col_scales(1)
     gather_col_segment(1)
-    largest = product(vc, cols_s, blt, res_d)
+    largest = product(vc, 1, blt, res_d)
     exchange_rows(1, largest)
     total = reduce_finish(0)
     at_cols = columns(total, 0)
@@ -434,35 +460,28 @@
     tile = gram(wb, wb, K, tile)
     reduce_start(1, tile)
 
-    wait_bytes(first_r.at[pl.ds(0, NR - 1)], send_sem.at[18])
-    wait_bytes(first_c.at[pl.ds(0, NC - 1)], send_sem.at[19])
-    wait_bytes(ar.at[0, pl.ds(0, NR * NC - 1)], send_sem.at[16])
-    for n in range(2):
-        for i, (ref, count) in enumerate(
-            [
-                (seg_sr, NC), (seg_qr, NC), (seg_sc, NR), (seg_qc, NR),
-                (in_sc, NR), (in_c, NR), (in_sr, NC), (in_r, NC),
-            ]
-        ):
-            wait_bytes(ref.at[n, pl.ds(0, count - 1)], send_sem.at[8 * n + i])
-
     total = reduce_finish(1)
     at_cols = columns(total, 0)
     s_cols = columns(total, K)
     a2_cols = rows_of(total)
     ata = matmul_cols(at_cols, a2_cols)
+    for b in range(M):
+        wb[b] = wb[b] - apply(at_cols, q2, b)
+    order_root = math.sqrt(NR * NC * M * LANES)
     inverse, _, _ = factor([s - t for s, t in zip(s_cols, ata)])
-    back = matmul_cols(inverse, at_cols)
-    order_root = math.sqrt(NR * NC * M * LANES)
-    for b in range(M):
-        value = apply(inverse, wb, b) - apply(back, q2, b)
-        next_out[:, pl.ds(LANES * b, LANES)] = value * order_root
+    inverse = [v * order_root for v in inverse]
+    for b in range(M):
+        next_out[:, pl.ds(LANES * b, LANES)] = apply(inverse, wb, b)
     low = zero
     for j in range(K):
         low = jnp.where(lane_iota == j, upper1[j], low)
         low = jnp.where(lane_iota == K + j, a2_cols[j], low)
     tri_out[pl.ds(K, K), :] = low[:, : 2 * K]
-    wait_bytes(ar.at[1, pl.ds(0, NR * NC - 1)], send_sem.at[17])
+
+    sent = 2 * (2 * (NC - 1) + NR - 1)
+    wait_bytes(bl.at[pl.ds(0, sent // 2)], send_sem.at[0])
+    wait_bytes(res_d.at[pl.ds(0, sent + 2 * (NR * NC - 1))], send_sem.at[1])
+    wait_bytes(ar.at[0, pl.ds(0, NR + NC - 2)], send_sem.at[2])
 
 
 def write_out(block, projection, block_out, projection_out, sems):
@@ -494,11 +513,9 @@
             pltpu.VMEM((SLOTS, LANES, LANES), BF16),
             pltpu.VMEM((SLOTS, LANES, LANES), BF16),
             pltpu.VMEM((K, M * LANES), F32),
-            pltpu.SMEM((1, SLOTS), jnp.int32),
-            pltpu.SMEM((1, SLOTS), jnp.int32),
+            pltpu.SMEM((2, 1, SLOTS), jnp.int32),
             pltpu.SMEM((NC, NR), jnp.int32),
-            pltpu.VMEM((1, SLOTS), jnp.int32),
-            pltpu.VMEM((1, SLOTS), jnp.int32),
+            pltpu.VMEM((2, 1, SLOTS), jnp.int32),
             *[pltpu.VMEM((M, *tile), F32)] * 7,
             pltpu.VMEM((2, M // 2, *pair), I16),
             pltpu.VMEM((2, 1, LANES), F32),
@@ -512,8 +529,8 @@
             pltpu.VMEM((RB, 2 * SLOTS), BF16),
             pltpu.VMEM((CB, 2 * SLOTS), BF16),
             pltpu.VMEM((2, *tile), F32),
-            pltpu.VMEM((K * SLOTS, LANES), F32),
-            pltpu.VMEM((K * SLOTS, LANES), F32),
+            pltpu.VMEM((K * PITCH, LANES), F32),
+            pltpu.VMEM((K * PITCH, LANES), F32),
             pltpu.VMEM((2, NC, K // 2, *pair), I16),
             pltpu.VMEM((2, NR, K // 2, *pair), I16),
             pltpu.VMEM((2, 1, LANES), F32),
@@ -528,7 +545,7 @@
             pltpu.VMEM((2, 1, LANES), F32),
             pltpu.VMEM((NR, 1, LANES), F32),
             pltpu.VMEM((NC, 1, LANES), F32),
-            pltpu.SemaphoreType.DMA((10,)),
+            pltpu.SemaphoreType.DMA((5,)),
             pltpu.SemaphoreType.DMA((20,)),
             pltpu.SemaphoreType.DMA((20,)),
         ],

time: 39.5 us -> 39.4 us (level)
  no operation moved by 1% of the time
where the time goes in v6:
time: 39.4 us; the launch traced here: 39.2 us
  Pallas kernels  38.6 us (98%)
  between operations  0.64 us (2%)
    pallas_call x1, Pallas kernels, per_device(): pl.pallas_call(kernel, out_shape=(jax.ShapeDtypeStruct((K, M * LANES), F3...  38 us

profile of v6, /device:TPU:1, one launch (start us, length us, event | category | flops | bytes accessed | tf_op | source)
XLA Modules:
  0.0 39.2 jit_solution(16217574144044791362)
XLA Ops:
  0.6 38.0 %lanczos.1 = (f32[8,1024]{1,0:T(8,128)S(1)}, f32[16,16]{1,0:T(8,128)S(1)}) custom-call(f32[8,1024]{1,0:T(8,128)} %x_hbm.1, bf16[1,1,128,128,128]{4,3,2,1,0:T(8,128)(2,1)} %blocks.1, s32[16,1,128]{2,1,0:T(1,128)} %rows_hbm.1, s32[16,1,128]{2,1,0:T(1,128)} %cols_hbm.1, s32[8,16]{1,0:T(8,128)} %bitcast.1), custom_call_target="tpu_custom_call" | custom-call | tf_op jit(solution)/shard_map/lanczos/pallas_call | solution.py:504
  38.6 0.6 %write_out.1 = (f32[8,1024]{1,0:T(8,128)}, f32[16,16]{1,0:T(8,128)}) custom-call(f32[8,1024]{1,0:T(8,128)S(1)} %get-tuple-element.4.block, f32[16,16]{1,0:T(8,128)S(1)} %get-tuple-element.5.projection), custom_call_target="tpu_custom_call" | custom-call | tf_op jit(solution)/shard_map/write_out/pallas_call | solution.py:557

commit v7 on v6

--- a/solution.py
+++ b/solution.py
@@ -241,9 +241,12 @@
         for cc in col_peers:
             send(own_q.at[n], seg_qr.at[n, c], 8 * n + 1, (r, cc))
         for rr in row_peers:
-            send_if(rr > r, own_s.at[n], seg_sc.at[n, r], 8 * n + 2, (rr, c))
-        for rr in row_peers:
-            send_if(rr > r, own_q.at[n], seg_qc.at[n, r], 8 * n + 3, (rr, c))
+
+            @pl.when(rr > r)
+            def _():
+                send(own_s.at[n], seg_sc.at[n, r], 8 * n + 2, (rr, c))
+                send(own_q.at[n], seg_qc.at[n, r], 8 * n + 3, (rr, c))
+
         seg_sr[n, c] = own_s[n]
         seg_qr[n, c] = own_q[n]
         seg_sc[n, r] = own_s[n]
@@ -321,11 +324,14 @@
     def exchange_cols(n, largest):
         inv, scale = scales(largest * most[1])
         sum_sc[n] = to_row(scale)
-        for rr in row_peers:
-            send_if(rr < r, sum_sc.at[n], in_sc.at[n, r], 8 * n + 4, (rr, c))
         scatter(picks_c, res_t, inv, tot_c.at[n], NR)
         for rr in row_peers:
-            send_if(rr < r, tot_c.at[n, rr], in_c.at[n, r], 8 * n + 5, (rr, c))
+
+            @pl.when(rr < r)
+            def _():
+                send(sum_sc.at[n], in_sc.at[n, r], 8 * n + 4, (rr, c))
+                send(tot_c.at[n, rr], in_c.at[n, r], 8 * n + 5, (rr, c))
+
         in_sc[n, r] = sum_sc[n]
         in_c[n, r] = tot_c[n, r]
 
@@ -529,8 +535,8 @@
             pltpu.VMEM((RB, 2 * SLOTS), BF16),
             pltpu.VMEM((CB, 2 * SLOTS), BF16),
             pltpu.VMEM((2, *tile), F32),
-            pltpu.VMEM((K * PITCH, LANES), F32),
-            pltpu.VMEM((K * PITCH, LANES), F32),
+            pltpu.VMEM(((K + 1) * PITCH, LANES), F32),
+            pltpu.VMEM(((K + 1) * PITCH, LANES), F32),
             pltpu.VMEM((2, NC, K // 2, *pair), I16),
             pltpu.VMEM((2, NR, K // 2, *pair), I16),
             pltpu.VMEM((2, 1, LANES), F32),
@@ -539,7 +545,7 @@
             pltpu.VMEM((2, NR, K // 2, *pair), I16),
             pltpu.VMEM((2, NC, 1, LANES), F32),
             pltpu.VMEM((2, NR, 1, LANES), F32),
-            pltpu.VMEM((K * M, LANES), F32),
+            pltpu.VMEM(((K + 1) * M, LANES), F32),
             pltpu.VMEM((2, 1, LANES), F32),
             pltpu.VMEM((2, NR * NC, 1, LANES), F32),
             pltpu.VMEM((2, 1, LANES), F32),

time: 39.4 us -> 39.3 us (level)
  no operation moved by 1% of the time
where the time goes in v7:
time: 39.3 us; the launch traced here: 39.2 us
  Pallas kernels  38.6 us (98%)
  between operations  0.64 us (2%)
    pallas_call x1, Pallas kernels, per_device(): pl.pallas_call(kernel, out_shape=(jax.ShapeDtypeStruct((K, M * LANES), F3...  37.9 us

profile of v7, /device:TPU:1, one launch (start us, length us, event | category | flops | bytes accessed | tf_op | source)
XLA Modules:
  0.0 39.2 jit_solution(6938256401810020098)
XLA Ops:
  0.6 37.9 %lanczos.1 = (f32[8,1024]{1,0:T(8,128)S(1)}, f32[16,16]{1,0:T(8,128)S(1)}) custom-call(f32[8,1024]{1,0:T(8,128)} %x_hbm.1, bf16[1,1,128,128,128]{4,3,2,1,0:T(8,128)(2,1)} %blocks.1, s32[16,1,128]{2,1,0:T(1,128)} %rows_hbm.1, s32[16,1,128]{2,1,0:T(1,128)} %cols_hbm.1, s32[8,16]{1,0:T(8,128)} %bitcast.1), custom_call_target="tpu_custom_call" | custom-call | tf_op jit(solution)/shard_map/lanczos/pallas_call | solution.py:510
  38.6 0.6 %write_out.1 = (f32[8,1024]{1,0:T(8,128)}, f32[16,16]{1,0:T(8,128)}) custom-call(f32[8,1024]{1,0:T(8,128)S(1)} %get-tuple-element.4.block, f32[16,16]{1,0:T(8,128)S(1)} %get-tuple-element.5.projection), custom_call_target="tpu_custom_call" | custom-call | tf_op jit(solution)/shard_map/write_out/pallas_call | solution.py:563
